TPU v7x, 32 devices: a whole 2x2x4 slice. The times are simulated.
32 devices in a mesh: north: 8 (over y, x, core), deep: 4 (over z).
Axes of the slice: x: 2, y: 2, z: 4, core: 2. Of those that a mesh axis runs over, the one named last changes fastest.
Arguments:
- forcing: float32 [2, 128, 128, 256], P(None, None, 'north', 'deep'), may hold values from -6 to 6
- symbol_x: float32 [128], replicated, may hold values from 0.3 to 3
- symbol_y: float32 [128], replicated, may hold values from 0.3 to 3
- symbol_z: float32 [256], replicated, may hold values from 0.3 to 3
Outputs:
- coefficients: float32 [2, 128, 128, 256], P(None, 'north', 'deep')
All inputs are finite; a program needn't handle non-finite values.
Results may differ from a plain program's by a relative error of at most 0.000084.
Values sent between devices are 32-bit elements; how exact they have to be, the bound alone decides.
No kernel may reach another device: no remote copies, remote signals or barrier semaphores. Data moves between devices by JAX's collectives and lax.ppermute only.
A program may use at most 64 MiB of HBM per device.

v0:
```python
import functools

import jax
import jax.numpy as jnp
import numpy as np
from jax import lax
from jax.experimental import pallas as pl
from jax.experimental.pallas import tpu as pltpu
from jax.sharding import PartitionSpec as P


VMEM = pltpu.VMEM
F32, BF16 = jnp.float32, jnp.bfloat16
SHARES = (6, 10)


def transform_table(count):
    rank = np.arange(count)
    steps = (2 * rank[:, None] + 1) * (2 * rank[None, :] + 1) % (8 * count)
    table = np.cos(np.pi / (4 * count) * steps) * (2.0 / count) ** 0.5
    high = table.astype(np.float32).astype(BF16)
    low = (table - high.astype(np.float64)).astype(np.float32).astype(BF16)
    return high, low


def split(values):
    high = values.astype(BF16)
    return high, (values - high.astype(F32)).astype(BF16)


def dot(a, b, dims):
    return lax.dot_general(a, b, (dims, ((), ())), preferred_element_type=F32)


def dot3(a, b, dims):
    return dot(a[0], b[0], dims) + (dot(a[0], b[1], dims) + dot(a[1], b[0], dims))


NORTH_KEY = (lambda s: s, lambda s: s)
NEAR_BYTES = 2**20


def near(fits, array):
    return pltpu.with_memory_space_constraint(array, VMEM) if fits else array


def block(fits, shape, dtype=F32):
    return VMEM(shape, dtype) if fits else jax.ShapeDtypeStruct(shape, dtype)


def partner(index, step, count):
    return index ^ step if count & (count - 1) == 0 else lax.rem(index + step, count)


def source(index, step, count):
    return index ^ step if count & (count - 1) == 0 else lax.rem(index + count - step, count)


def call(kernel, outs, cost, aliases=None, scratch=(), in_specs=None, out_specs=None):
    flops, moved = cost
    kwargs = {}
    if in_specs is not None:
        kwargs["in_specs"] = in_specs
    if out_specs is not None:
        kwargs["out_specs"] = out_specs
    return pl.pallas_call(
        kernel,
        out_shape=outs,
        input_output_aliases=aliases or {},
        scratch_shapes=scratch,
        cost_estimate=pl.CostEstimate(flops=int(flops), bytes_accessed=int(moved), transcendentals=0),
        **kwargs,
    )


def dot_stacked(a, a_high, b, dims):
    rows = a_high.shape[0]
    both = dot(a, b[0], dims)
    return both[:rows] + (both[rows:] + dot(a_high, b[1], dims))


def x_kernel(inner, outer, chunks, *refs):
    field, high, low = refs[:3]
    tables, outs = refs[3 : 3 + len(chunks)], refs[3 + len(chunks) :]
    me = lax.axis_index("north")
    chip, core = me // inner, lax.rem(me, inner)
    shares = [ref[partner(chip, s, outer), core] for ref in (high, low) for s in range(outer)]
    table = jnp.concatenate(shares, 0).astype(BF16)
    for (first, last, _, _), ref in zip(chunks, tables):
        ref[...] = jnp.concatenate([rows[first:last] for rows in shares], 0).astype(BF16)
    for y, s, value in line_modes(field, table, outer):
        for c, (_, _, start, count) in enumerate(chunks):
            outs[c * outer + s][pl.ds(y, count, stride=field.shape[1]), :] = value[start : start + count]


def line_modes(field, table, outer):
    fields, lines = field.shape[:2]
    rows = table.shape[0] // 2
    share = rows // outer
    table_high = table[:rows]
    pair = 2 if lines % 2 == 0 else 1
    for y in range(0, lines, pair):
        columns = jnp.concatenate([field[f, y + i] for i in range(pair) for f in range(fields)], 0)
        modes = dot_stacked(table, table_high, split(columns), ((1,), (1,)))
        lanes = modes.shape[1] // pair
        for i in range(pair):
            for s in range(outer):
                yield y + i, s, modes[s * share : (s + 1) * share, i * lanes : (i + 1) * lanes]


def other_kernel(outer, count, skip, *refs):
    field, table, before, outs = refs[0], refs[1], refs[2:-outer], refs[-outer:]
    lines = field.shape[1]
    done = before[0].shape[0] // (count * lines) if before else 0
    join(count, [before], outs)
    for y, s, value in line_modes(field, table[...], outer):
        outs[s][pl.ds(done * lines + y, count, stride=(done + 1) * lines), :] = value[skip : skip + count]


def join(count, groups, outs):
    total = outs[0].shape[0] // count
    at = 0
    for blocks in groups:
        for block, out in zip(blocks, outs):
            size = block.shape[0] // count
            for r in range(count):
                out[pl.ds(r * total + at, size), :] = block[pl.ds(r * size, size), :]
        at += blocks[0].shape[0] // count if blocks else 0


def join_kernel(count, outer, *refs):
    join(count, (refs[:outer], refs[outer : 2 * outer]), refs[2 * outer :])


def y_kernel(inner, outer, deep, order, *refs):
    parts, (high, low), outs = refs[:outer], refs[outer : outer + 2], refs[outer + 2 : outer + 2 + deep]
    terms = refs[outer + 2 + deep :]
    me, layer = lax.axis_index("north"), lax.axis_index("deep")
    chip, core = me // inner, lax.rem(me, inner)
    count, share, _ = outs[0].shape
    lines = parts[0].shape[0] // (count * inner)
    table = jnp.concatenate(
        [ref[pl.ds(pl.multiple_of(partner(layer, s, deep) * share, share), share), :] for ref in (high, low) for s in range(deep)],
        0,
    )
    table_high = table[: share * deep]
    lanes = parts[0].shape[1]
    for r in range(count):
        for part, s in zip(parts, (0, *order)):
            for k in range(inner):
                at = (source(chip, s, outer) * inner + source(core, k, inner)) * lines
                at = pl.multiple_of(at, lines)
                for term, value in zip(terms, split(part[pl.ds((r * inner + k) * lines, lines), :])):
                    term[pl.ds(at, lines), r * lanes : (r + 1) * lanes] = value
    for r in range(0, count, 2):
        group = range(r, min(r + 2, count))
        columns = tuple(term[:, r * lanes : (group[-1] + 1) * lanes] for term in terms)
        modes = dot_stacked(table, table_high, columns, ((1,), (0,)))
        for i in group:
            for s in range(deep):
                outs[s][i] = modes[s * share : (s + 1) * share, (i - r) * lanes : (i - r + 1) * lanes]


def z_kernel(fields, steps, deep, start, *refs):
    high, low, factor = refs[len(steps) : len(steps) + 3]
    out, stage, sems = refs[-3:]
    order = tuple(dict.fromkeys(steps))
    parts = [[ref for ref, s in zip(refs, steps) if s == step] for step in order]
    layer = lax.axis_index("deep")
    count, modes_y, lanes = refs[0].shape
    depth = lanes // fields
    table = tuple(
        jnp.concatenate([ref[pl.ds(pl.multiple_of(source(layer, s, deep) * depth, depth), depth), :] for s in order], 0)
        for ref in (high, low)
    )
    rows = count * modes_y
    pieces = [split(sum(ref[...] for ref in part).reshape(rows, lanes)) for part in parts]
    copies = []
    for f in range(fields):
        lines = tuple(
            jnp.concatenate([piece[term][:, f * depth : (f + 1) * depth] for piece in pieces], 1) for term in range(2)
        )
        modes = dot3(lines, table, ((1,), (0,)))
        stage[f] = modes.reshape(count, modes_y, modes.shape[1]) * factor[start : start + count]
        copy = pltpu.make_async_copy(stage.at[f], out.at[f, pl.ds(start, count)], sems.at[f])
        copy.start()
        copies.append(copy)
    for copy in copies:
        copy.wait()


def local(north, deep, forcing, symbol_x, symbol_y, symbol_z):
    fields, size_x, lines, depth = forcing.shape
    size_y, size_z = lines * north, depth * deep
    inner = 2 if north % 2 == 0 else 1
    outer = north // inner
    share_x, share_y = size_x // north, size_y // deep
    lanes = fields * depth
    hold = functools.partial(near, 4 * forcing.size <= NEAR_BYTES)
    made = functools.partial(block, 4 * forcing.size <= NEAR_BYTES)
    ends = np.rint(np.cumsum((0,) + SHARES) / sum(SHARES) * share_x).astype(int)
    chunks = tuple(int(n) for n in np.diff(ends) if n > 0)

    tables = {n: transform_table(n) for n in {size_x, size_y, size_z}}
    table_x = [jnp.asarray(t.astype(np.float32).reshape(outer, inner, share_x, size_x)) for t in tables[size_x]]
    table_y = [jnp.asarray(t) for t in tables[size_y]]
    table_z = [jnp.asarray(t) for t in tables[size_z]]

    field = jnp.transpose(forcing, (0, 2, 3, 1))
    cost_x = (2 * field.size * outer * share_x * 3, 8 * field.size)
    spans, start = [], 0
    for count in chunks:
        spans.append((start // 8 * 8, min(-(-(start + count) // 8) * 8, share_x), start, count))
        start += count
    sends = [made((2 * outer * (last - first), size_x), BF16) for first, last, _, _ in spans]
    sends += [made((count * lines, lanes)) for count in chunks for _ in range(outer)]
    own = call(functools.partial(x_kernel, inner, outer, spans), tuple(sends), cost_x)(field, *table_x)
    ready_x, own = own[: len(chunks)], own[len(chunks) :]
    buffers = [own[c * outer : (c + 1) * outer] for c in range(len(chunks))]
    for k in range(1, inner):
        pairs = [(j, j // inner * inner + partner_int(j % inner, k, inner)) for j in range(north)]
        taken = hold(lax.ppermute(field, "north", pairs))
        for c, (first, last, start, count) in enumerate(spans):
            together = buffers[c] if c == 0 else ()
            other = call(
                functools.partial(other_kernel, outer, count, start - first),
                tuple(made((count * (k + 1 if together else 1) * lines, lanes)) for _ in range(outer)),
                (cost_x[0] * count // share_x, cost_x[1]),
            )(taken, hold(ready_x[c]), *map(hold, together))
            if not together:
                other = call(
                    functools.partial(join_kernel, count, outer),
                    tuple(made((count * (k + 1) * lines, lanes)) for _ in range(outer)),
                    (1000, 16 * outer * count * lines * lanes),
                )(*map(hold, buffers[c]), *map(hold, other))
            buffers[c] = other

    symbol_x, symbol_y, symbol_z, buffers[0] = lax.optimization_barrier((symbol_x, symbol_y, symbol_z, buffers[0]))
    part_x = lax.dynamic_slice_in_dim(symbol_x, lax.axis_index("north") * share_x, share_x)
    part_y = lax.dynamic_slice_in_dim(symbol_y, lax.axis_index("deep") * share_y, share_y)
    symbol = part_x[:, None, None] + part_y[None, :, None] + symbol_z[None, None, :]
    factor = (1.0 - 0.2 * symbol) / (1.0 + 0.2 * symbol)

    result, start = (), 0
    for c, count in enumerate(chunks):
        north_order = sorted(range(1, outer), key=NORTH_KEY[min(c, 1)])
        parts = list(buffers[c])
        for s in north_order:
            pairs = [(j, partner_int(j // inner, s, outer) * inner + j % inner) for j in range(north)]
            parts[s] = lax.ppermute(parts[s], "north", pairs)
        cost_y = (2 * count * size_y * size_y * lanes * 3, 8 * count * size_y * lanes)
        blocks = call(
            functools.partial(y_kernel, inner, outer, deep, north_order),
            tuple(made((count, share_y, lanes)) for _ in range(deep)),
            cost_y,
            scratch=(VMEM((size_y, count * lanes), BF16), VMEM((size_y, count * lanes), BF16)),
        )(*[hold(parts[s]) for s in (0, *north_order)], *map(hold, table_y))
        sends_z = deep_sends(deep, c)
        steps_z = (0,) + tuple(s for s, _ in sends_z)
        gathered = [blocks[0]] + [lax.ppermute(blocks[s], "deep", pairs) for s, pairs in sends_z]
        shape = (fields, share_x, share_y, size_z)
        cost_z = (2 * count * share_y * size_z * size_z * fields * 3, 8 * count * share_y * size_z * fields)
        whole = pl.BlockSpec(memory_space=VMEM)
        anywhere = pl.BlockSpec(memory_space=pl.ANY)
        result = (
            call(
                functools.partial(z_kernel, fields, steps_z, deep, start),
                jax.ShapeDtypeStruct(shape, F32),
                cost_z,
                aliases={len(steps_z) + 3: 0} if c else {},
                scratch=(VMEM((fields, count) + shape[2:], F32), pltpu.SemaphoreType.DMA((fields,))),
                in_specs=[whole] * (len(steps_z) + 3) + [anywhere] * len(result),
                out_specs=anywhere,
            )(*map(hold, gathered), *map(hold, table_z), hold(factor), *result),
        )
        start += count
    return result[0]


def partner_int(index, step, count):
    return index ^ step if count & (count - 1) == 0 else (index + step) % count


def deep_sends(deep, chunk):
    steps = [(s, [(j, partner_int(j, s, deep)) for j in range(deep)]) for s in range(1, deep)]
    if deep != 4:
        return sorted(steps, key=lambda step: (-step[0].bit_length(), step[0]))
    (one, near), (two, across), (three, ends) = steps
    return [[(three, ends), (two, across), (one, near)], [(two, across), (three, ends), (one, near)]][min(chunk, 1)]


def solution(mesh):
    def step(*arrays):
        return local(mesh.shape["north"], mesh.shape["deep"], *arrays)

    placed = (P(None, None, "north", "deep"), P(), P(), P())
    return jax.shard_map(
        step, mesh=mesh, in_specs=placed, out_specs=P(None, "north", "deep", None), check_vma=False
    )
```

profile of v0, /device:TPU:10, one launch (start us, length us, event | category | flops | bytes accessed | tf_op | source)
XLA Modules:
  0.0 37.8 jit_solution(16112395622087105102)
XLA Ops:
  0.0 0.0 collective-permute-start
  0.0 1.8 %shard_map.100 = (bf16[64,128]{1,0:T(8,128)(2,1)S(1)}, bf16[128,128]{1,0:T(8,128)(2,1)S(1)}, f32[96,128]{1,0:T(8,128)S(1)}, f32[96,128]{1,0:T(8,128)S(1)}, f32[9...) custom-call(f32[2,16,64,128]{3,2,1,0:T(8,128)} %bitcast.2, ...), custom_call_target="tpu_custom_call" | custom-call | flops 100663296 | bytes 2097152 | tf_op jit(solution)/shard_map/pallas_call | solution.py:217
  1.8 1.1 %collective-permute-done.refs_0_ = f32[2,16,64,128]{3,2,1,0:T(8,128)S(1)} collective-permute-done((f32[2,16,64,128]{3,2,1,0:T(8,128)}, f32[2,16,64,128]{3,2,1,0:T(8,128)S(1)}, u32[]{:S(2)}, u32[]{:S(2)}) %collective-permute-start) | collective-permute-done | bytes 1048608 | tf_op jit(solution)/shard_map/ppermute | solution.py:222
  2.9 0.5 %shard_map.104 = (f32[192,128]{1,0:T(8,128)S(1)}, f32[192,128]{1,0:T(8,128)S(1)}, f32[192,128]{1,0:T(8,128)S(1)}, f32[192,128]{1,0:T(8,128)S(1)}) custom-call(f32[2,16,64,128]{3,2,1,0:T(8,128)S(1)} %collective-permute-done.refs_0_, bf16[64,128]{1,0:T(8,128)(2,1)S(1)} %get-tuple-element.59.refs_1_, f32[96,128]{1,0:T(8,128)S(1)} %get-tuple-element.60.refs_2_, ...), custom_call_target="tpu_custom_call" | custom-call | flops 37748736 | bytes 2097152 | tf_op jit(solution)/shard_map/pallas_call | solution.py:225
  3.4 0.6 %collective-permute-start.7 = (f32[192,128]{1,0:T(8,128)S(1)}, f32[192,128]{1,0:T(8,128)S(1)}, u32[]{:S(2)}, u32[]{:S(2)}) collective-permute-start(f32[192,128]{1,0:T(8,128)S(1)} %get-tuple-element.72), channel_id=1, source_target_pairs={{0,8},{4,12},{8,0},{12,4},{16,24},{20,28},{24,16},{28,20},{1,9},{5... | collective-permute-start | bytes 294920 | tf_op jit(solution)/shard_map/ppermute | solution.py:250
  4.0 1.5 %collective-permute-start.8 = (f32[192,128]{1,0:T(8,128)S(1)}, f32[192,128]{1,0:T(8,128)S(1)}, u32[]{:S(2)}, u32[]{:S(2)}) collective-permute-start(f32[192,128]{1,0:T(8,128)S(1)} %get-tuple-element.73), channel_id=1, source_target_pairs={{0,16},{4,20},{8,24},{12,28},{16,0},{20,4},{24,8},{28,12},{1,17},{... | collective-permute-start | bytes 294920 | tf_op jit(solution)/shard_map/ppermute | solution.py:250
  5.5 1.4 %collective-permute-start.9 = (f32[192,128]{1,0:T(8,128)S(1)}, f32[192,128]{1,0:T(8,128)S(1)}, u32[]{:S(2)}, u32[]{:S(2)}) collective-permute-start(f32[192,128]{1,0:T(8,128)S(1)} %get-tuple-element.74), channel_id=1, source_target_pairs={{0,24},{4,28},{8,16},{12,20},{16,8},{20,12},{24,0},{28,4},{1,25},{... | collective-permute-start | bytes 294920 | tf_op jit(solution)/shard_map/ppermute | solution.py:250
  6.9 0.5 %shard_map.101 = (f32[160,128]{1,0:T(8,128)S(1)}, f32[160,128]{1,0:T(8,128)S(1)}, f32[160,128]{1,0:T(8,128)S(1)}, f32[160,128]{1,0:T(8,128)S(1)}) custom-call(f32[2,16,64,128]{3,2,1,0:T(8,128)S(1)} %collective-permute-done.refs_0_, bf16[128,128]{1,0:T(8,128)(2,1)S(1)} %get-tuple-element.46.refs_1_), custom_call_target="tpu_custom_call" | custom-call | flops 62914560 | bytes 2097152 | tf_op jit(solution)/shard_map/pallas_call | solution.py:225
  7.4 0.0 copy-start.2
  7.4 0.0 copy-start.3
  7.5 0.0 copy-start.5
  7.5 0.6 %collective-permute-start.1 = (f32[320,128]{1,0:T(8,128)S(1)}, f32[320,128]{1,0:T(8,128)S(1)}, u32[]{:S(2)}, u32[]{:S(2)}) collective-permute-start(f32[320,128]{1,0:T(8,128)S(1)} %get-tuple-element.52), channel_id=1, source_target_pairs={{0,8},{4,12},{8,0},{12,4},{16,24},{20,28},{24,16},{28,20},{1,9},{5... | collective-permute-start | bytes 491528 | tf_op jit(solution)/shard_map/ppermute | solution.py:250
  8.1 1.5 %collective-permute-start.2 = (f32[320,128]{1,0:T(8,128)S(1)}, f32[320,128]{1,0:T(8,128)S(1)}, u32[]{:S(2)}, u32[]{:S(2)}) collective-permute-start(f32[320,128]{1,0:T(8,128)S(1)} %get-tuple-element.53), channel_id=1, source_target_pairs={{0,16},{4,20},{8,24},{12,28},{16,0},{20,4},{24,8},{28,12},{1,17},{... | collective-permute-start | bytes 491528 | tf_op jit(solution)/shard_map/ppermute | solution.py:250
  9.6 0.0 copy-done.5
  9.6 0.1 dynamic_slice.6
  9.7 0.0 copy-done.6
  9.7 0.1 dynamic_slice.7
  9.8 0.0 collective-permute-done.7.refs_1_
  9.8 1.5 %collective-permute-start.3 = (f32[320,128]{1,0:T(8,128)S(1)}, f32[320,128]{1,0:T(8,128)S(1)}, u32[]{:S(2)}, u32[]{:S(2)}) collective-permute-start(f32[320,128]{1,0:T(8,128)S(1)} %get-tuple-element.54), channel_id=1, source_target_pairs={{0,24},{4,28},{8,16},{12,20},{16,8},{20,12},{24,0},{28,4},{1,25},{... | collective-permute-start | bytes 491528 | tf_op jit(solution)/shard_map/ppermute | solution.py:250
  11.3 0.0 collective-permute-done.8.refs_2_
  11.3 0.8 %collective-permute-done.9.refs_3_ = f32[192,128]{1,0:T(8,128)S(1)} collective-permute-done((f32[192,128]{1,0:T(8,128)S(1)}, f32[192,128]{1,0:T(8,128)S(1)}, u32[]{:S(2)}, u32[]{:S(2)}) %collective-permute-start.9) | collective-permute-done | bytes 98336 | tf_op jit(solution)/shard_map/ppermute | solution.py:250
  12.1 0.0 copy-done.2
  12.1 0.0 copy-done.3
  12.1 0.4 shard_map.105
  12.4 1.6 %collective-permute-start.10 = (f32[6,32,128]{2,1,0:T(8,128)S(1)}, f32[6,32,128]{2,1,0:T(8,128)S(1)}, u32[]{:S(2)}, u32[]{:S(2)}) collective-permute-start(f32[6,32,128]{2,1,0:T(8,128)S(1)} %get-tuple-element.76), channel_id=1, source_target_pairs={{0,3},{1,2},{2,1},{3,0},{4,7},{5,6},{6,5},{7,4},{8,11},{9,10},{10,... | collective-permute-start | bytes 294920 | tf_op jit(solution)/shard_map/ppermute | solution.py:260
  14.1 0.1 broadcast_add_fusion
  14.1 1.2 %collective-permute-start.11 = (f32[6,32,128]{2,1,0:T(8,128)S(1)}, f32[6,32,128]{2,1,0:T(8,128)S(1)}, u32[]{:S(2)}, u32[]{:S(2)}) collective-permute-start(f32[6,32,128]{2,1,0:T(8,128)S(1)} %get-tuple-element.77), channel_id=1, source_target_pairs={{0,2},{1,3},{2,0},{3,1},{4,6},{5,7},{6,4},{7,5},{8,10},{9,11},{10,... | collective-permute-start | bytes 294920 | tf_op jit(solution)/shard_map/ppermute | solution.py:260
  15.4 0.0 collective-permute-done.1.refs_1_
  15.4 1.3 %collective-permute-start.12 = (f32[6,32,128]{2,1,0:T(8,128)S(1)}, f32[6,32,128]{2,1,0:T(8,128)S(1)}, u32[]{:S(2)}, u32[]{:S(2)}) collective-permute-start(f32[6,32,128]{2,1,0:T(8,128)S(1)} %get-tuple-element.78), channel_id=1, source_target_pairs={{0,1},{1,0},{2,3},{3,2},{4,5},{5,4},{6,7},{7,6},{8,9},{9,8},{10,11... | collective-permute-start | bytes 294920 | tf_op jit(solution)/shard_map/ppermute | solution.py:260
  16.7 0.1 collective-permute-done.2.refs_2_
  16.8 1.6 %collective-permute-done.3.refs_3_ = f32[320,128]{1,0:T(8,128)S(1)} collective-permute-done((f32[320,128]{1,0:T(8,128)S(1)}, f32[320,128]{1,0:T(8,128)S(1)}, u32[]{:S(2)}, u32[]{:S(2)}) %collective-permute-start.3) | collective-permute-done | bytes 163872 | tf_op jit(solution)/shard_map/ppermute | solution.py:250
  18.4 0.5 %shard_map.103 = (f32[10,32,128]{2,1,0:T(8,128)S(1)}, f32[10,32,128]{2,1,0:T(8,128)S(1)}, f32[10,32,128]{2,1,0:T(8,128)S(1)}, f32[10,32,128]{2,1,0:T(8,128)S(1)}) custom-call(f32[320,128]{1,0:T(8,128)S(1)} %get-tuple-element.51.refs_0_, f32[320,128]{1,0:T(8,128)S(1)} %collective-permute-done.1.refs_1_, f32[320,128]{1,0:T(8,128)S(1)} %collective-permute-done.2.refs_2_, ...), custom_call_target="tpu_custom_call" | custom-call | flops 125829120 | bytes 1310720 | tf_op jit(solution)/shard_map/pallas_call | solution.py:252
  18.9 2.7 %collective-permute-start.4 = (f32[10,32,128]{2,1,0:T(8,128)S(1)}, f32[10,32,128]{2,1,0:T(8,128)S(1)}, u32[]{:S(2)}, u32[]{:S(2)}) collective-permute-start(f32[10,32,128]{2,1,0:T(8,128)S(1)} %get-tuple-element.56), channel_id=1, source_target_pairs={{0,2},{1,3},{2,0},{3,1},{4,6},{5,7},{6,4},{7,5},{8,10},{9,11},{10,... | collective-permute-start | bytes 491528 | tf_op jit(solution)/shard_map/ppermute | solution.py:260
  21.5 0.0 collective-permute-start.5
  21.5 0.0 collective-permute-done.10.refs_1_
  21.5 0.0 copy-start
  21.6 0.0 copy-start.1
  21.6 1.8 %collective-permute-start.6 = (f32[10,32,128]{2,1,0:T(8,128)S(1)}, f32[10,32,128]{2,1,0:T(8,128)S(1)}, u32[]{:S(2)}, u32[]{:S(2)}) collective-permute-start(f32[10,32,128]{2,1,0:T(8,128)S(1)} %get-tuple-element.58), channel_id=1, source_target_pairs={{0,1},{1,0},{2,3},{3,2},{4,5},{5,4},{6,7},{7,6},{8,9},{9,8},{10,11... | collective-permute-start | bytes 491528 | tf_op jit(solution)/shard_map/ppermute | solution.py:260
  23.3 0.0 copy-done.4
  23.4 0.2 add_divide_fusion.refs_6_
  23.5 4.0 %collective-permute-done.11.refs_2_ = f32[6,32,128]{2,1,0:T(8,128)S(1)} collective-permute-done((f32[6,32,128]{2,1,0:T(8,128)S(1)}, f32[6,32,128]{2,1,0:T(8,128)S(1)}, u32[]{:S(2)}, u32[]{:S(2)}) %collective-permute-start.11) | collective-permute-done | bytes 98336 | tf_op jit(solution)/shard_map/ppermute | solution.py:260
  27.5 0.0 collective-permute-done.12.refs_3_
  27.5 0.0 copy-done
  27.5 1.1 %shard_map.106.refs_7_ = f32[2,16,32,256]{3,2,1,0:T(8,128)} custom-call(f32[6,32,128]{2,1,0:T(8,128)S(1)} %get-tuple-element.75.refs_0_, f32[6,32,128]{2,1,0:T(8,128)S(1)} %collective-permute-done.10.refs_1_, f32[6,32,128]{2,1,0:T(8,128)S(1)} %collective-permute-done.11.refs_2_, f32[6,32,128]{2,1,0:T(8,128)S(1)} %collective-permute-done.12.refs_3_, ...), custom_call_target="tpu_custom_call" | custom-call | flops 150994944 | bytes 786432 | tf_op jit(solution)/shard_map/pallas_call | solution.py:266
  28.7 3.6 %collective-permute-done.4.refs_1_ = f32[10,32,128]{2,1,0:T(8,128)S(1)} collective-permute-done((f32[10,32,128]{2,1,0:T(8,128)S(1)}, f32[10,32,128]{2,1,0:T(8,128)S(1)}, u32[]{:S(2)}, u32[]{:S(2)}) %collective-permute-start.4) | collective-permute-done | bytes 163872 | tf_op jit(solution)/shard_map/ppermute | solution.py:260
  32.3 4.1 %collective-permute-done.5.refs_2_ = f32[10,32,128]{2,1,0:T(8,128)S(1)} collective-permute-done((f32[10,32,128]{2,1,0:T(8,128)S(1)}, f32[10,32,128]{2,1,0:T(8,128)S(1)}, u32[]{:S(2)}, u32[]{:S(2)}) %collective-permute-start.5) | collective-permute-done | bytes 163872 | tf_op jit(solution)/shard_map/ppermute | solution.py:260
  36.4 0.0 collective-permute-done.6.refs_3_
  36.4 1.3 %shard_map.107 = f32[2,16,32,256]{3,2,1,0:T(8,128)} custom-call(f32[10,32,128]{2,1,0:T(8,128)S(1)} %get-tuple-element.55.refs_0_, f32[10,32,128]{2,1,0:T(8,128)S(1)} %collective-permute-done.4.refs_1_, f32[10,32,128]{2,1,0:T(8,128)S(1)} %collective-permute-done.5.refs_2_, ...), custom_call_target="tpu_custom_call", output_to_operand_aliasing={{}: (7, {})} | custom-call | flops 251658240 | bytes 1310720 | tf_op jit(solution)/shard_map/pallas_call | solution.py:266
  (4 shorter events, 0.1 us)
Async XLA Ops:
  0.0 2.9 %collective-permute-start = (f32[2,16,64,128]{3,2,1,0:T(8,128)}, f32[2,16,64,128]{3,2,1,0:T(8,128)S(1)}, u32[]{:S(2)}, u32[]{:S(2)}) collective-permute-start(f32[2,16,64,128]{3,2,1,0:T(8,128)} %bitcast.1), channel_id=1, source_target_pairs={{0,4},{4,0},{8,12},{12,8},{16,20},{20,16},{24,28},{28,24},{1,5},{5... | collective-permute-start | bytes 3145736 | tf_op jit(solution)/shard_map/ppermute | solution.py:222
  3.4 6.4 %collective-permute-start.7 = (f32[192,128]{1,0:T(8,128)S(1)}, f32[192,128]{1,0:T(8,128)S(1)}, u32[]{:S(2)}, u32[]{:S(2)}) collective-permute-start(f32[192,128]{1,0:T(8,128)S(1)} %get-tuple-element.72), channel_id=1, source_target_pairs={{0,8},{4,12},{8,0},{12,4},{16,24},{20,28},{24,16},{28,20},{1,9},{5... | collective-permute-start | bytes 294920 | tf_op jit(solution)/shard_map/ppermute | solution.py:250
  4.0 7.3 %collective-permute-start.8 = (f32[192,128]{1,0:T(8,128)S(1)}, f32[192,128]{1,0:T(8,128)S(1)}, u32[]{:S(2)}, u32[]{:S(2)}) collective-permute-start(f32[192,128]{1,0:T(8,128)S(1)} %get-tuple-element.73), channel_id=1, source_target_pairs={{0,16},{4,20},{8,24},{12,28},{16,0},{20,4},{24,8},{28,12},{1,17},{... | collective-permute-start | bytes 294920 | tf_op jit(solution)/shard_map/ppermute | solution.py:250
  5.5 6.6 %collective-permute-start.9 = (f32[192,128]{1,0:T(8,128)S(1)}, f32[192,128]{1,0:T(8,128)S(1)}, u32[]{:S(2)}, u32[]{:S(2)}) collective-permute-start(f32[192,128]{1,0:T(8,128)S(1)} %get-tuple-element.74), channel_id=1, source_target_pairs={{0,24},{4,28},{8,16},{12,20},{16,8},{20,12},{24,0},{28,4},{1,25},{... | collective-permute-start | bytes 294920 | tf_op jit(solution)/shard_map/ppermute | solution.py:250
  7.4 4.6 %copy-start.2 = (bf16[128,128]{1,0:T(8,128)(2,1)S(1)}, bf16[128,128]{1,0:T(8,128)(2,1)}, u32[]{:S(2)}) copy-start(bf16[128,128]{1,0:T(8,128)(2,1)} %constant.36.clone.refs_5_) | copy-start | bytes 98308
  7.4 4.6 %copy-start.3 = (bf16[128,128]{1,0:T(8,128)(2,1)S(1)}, bf16[128,128]{1,0:T(8,128)(2,1)}, u32[]{:S(2)}) copy-start(bf16[128,128]{1,0:T(8,128)(2,1)} %constant.35.clone.refs_4_) | copy-start | bytes 98308
  7.5 2.1 %copy-start.5 = (f32[128]{0:T(128)S(1)}, f32[128]{0:T(128)}, u32[]{:S(2)}) copy-start(f32[128]{0:T(128)} %param.11) | copy-start | bytes 1540
  7.5 7.9 %collective-permute-start.1 = (f32[320,128]{1,0:T(8,128)S(1)}, f32[320,128]{1,0:T(8,128)S(1)}, u32[]{:S(2)}, u32[]{:S(2)}) collective-permute-start(f32[320,128]{1,0:T(8,128)S(1)} %get-tuple-element.52), channel_id=1, source_target_pairs={{0,8},{4,12},{8,0},{12,4},{16,24},{20,28},{24,16},{28,20},{1,9},{5... | collective-permute-start | bytes 491528 | tf_op jit(solution)/shard_map/ppermute | solution.py:250
  8.1 1.6 %copy-start.6 = (f32[128]{0:T(128)S(1)}, f32[128]{0:T(128)}, u32[]{:S(2)}) copy-start(f32[128]{0:T(128)} %param.12) | copy-start | bytes 1540
  8.1 8.7 %collective-permute-start.2 = (f32[320,128]{1,0:T(8,128)S(1)}, f32[320,128]{1,0:T(8,128)S(1)}, u32[]{:S(2)}, u32[]{:S(2)}) collective-permute-start(f32[320,128]{1,0:T(8,128)S(1)} %get-tuple-element.53), channel_id=1, source_target_pairs={{0,16},{4,20},{8,24},{12,28},{16,0},{20,4},{24,8},{28,12},{1,17},{... | collective-permute-start | bytes 491528 | tf_op jit(solution)/shard_map/ppermute | solution.py:250
  9.8 8.6 %collective-permute-start.3 = (f32[320,128]{1,0:T(8,128)S(1)}, f32[320,128]{1,0:T(8,128)S(1)}, u32[]{:S(2)}, u32[]{:S(2)}) collective-permute-start(f32[320,128]{1,0:T(8,128)S(1)} %get-tuple-element.54), channel_id=1, source_target_pairs={{0,24},{4,28},{8,16},{12,20},{16,8},{20,12},{24,0},{28,4},{1,25},{... | collective-permute-start | bytes 491528 | tf_op jit(solution)/shard_map/ppermute | solution.py:250
  12.4 9.1 %collective-permute-start.10 = (f32[6,32,128]{2,1,0:T(8,128)S(1)}, f32[6,32,128]{2,1,0:T(8,128)S(1)}, u32[]{:S(2)}, u32[]{:S(2)}) collective-permute-start(f32[6,32,128]{2,1,0:T(8,128)S(1)} %get-tuple-element.76), channel_id=1, source_target_pairs={{0,3},{1,2},{2,1},{3,0},{4,7},{5,6},{6,5},{7,4},{8,11},{9,10},{10,... | collective-permute-start | bytes 294920 | tf_op jit(solution)/shard_map/ppermute | solution.py:260
  14.1 13.4 %collective-permute-start.11 = (f32[6,32,128]{2,1,0:T(8,128)S(1)}, f32[6,32,128]{2,1,0:T(8,128)S(1)}, u32[]{:S(2)}, u32[]{:S(2)}) collective-permute-start(f32[6,32,128]{2,1,0:T(8,128)S(1)} %get-tuple-element.77), channel_id=1, source_target_pairs={{0,2},{1,3},{2,0},{3,1},{4,6},{5,7},{6,4},{7,5},{8,10},{9,11},{10,... | collective-permute-start | bytes 294920 | tf_op jit(solution)/shard_map/ppermute | solution.py:260
  15.4 12.1 %collective-permute-start.12 = (f32[6,32,128]{2,1,0:T(8,128)S(1)}, f32[6,32,128]{2,1,0:T(8,128)S(1)}, u32[]{:S(2)}, u32[]{:S(2)}) collective-permute-start(f32[6,32,128]{2,1,0:T(8,128)S(1)} %get-tuple-element.78), channel_id=1, source_target_pairs={{0,1},{1,0},{2,3},{3,2},{4,5},{5,4},{6,7},{7,6},{8,9},{9,8},{10,11... | collective-permute-start | bytes 294920 | tf_op jit(solution)/shard_map/ppermute | solution.py:260
  18.9 13.4 %collective-permute-start.4 = (f32[10,32,128]{2,1,0:T(8,128)S(1)}, f32[10,32,128]{2,1,0:T(8,128)S(1)}, u32[]{:S(2)}, u32[]{:S(2)}) collective-permute-start(f32[10,32,128]{2,1,0:T(8,128)S(1)} %get-tuple-element.56), channel_id=1, source_target_pairs={{0,2},{1,3},{2,0},{3,1},{4,6},{5,7},{6,4},{7,5},{8,10},{9,11},{10,... | collective-permute-start | bytes 491528 | tf_op jit(solution)/shard_map/ppermute | solution.py:260
  21.5 1.8 %copy-start.4 = (f32[256]{0:T(256)S(1)}, f32[256]{0:T(256)}, u32[]{:S(2)}) copy-start(f32[256]{0:T(256)} %param.13) | copy-start | bytes 3076
  21.5 14.9 %collective-permute-start.5 = (f32[10,32,128]{2,1,0:T(8,128)S(1)}, f32[10,32,128]{2,1,0:T(8,128)S(1)}, u32[]{:S(2)}, u32[]{:S(2)}) collective-permute-start(f32[10,32,128]{2,1,0:T(8,128)S(1)} %get-tuple-element.57), channel_id=1, source_target_pairs={{0,3},{1,2},{2,1},{3,0},{4,7},{5,6},{6,5},{7,4},{8,11},{9,10},{10,... | collective-permute-start | bytes 491528 | tf_op jit(solution)/shard_map/ppermute | solution.py:260
  21.5 6.0 %copy-start = (bf16[256,256]{1,0:T(8,128)(2,1)S(1)}, bf16[256,256]{1,0:T(8,128)(2,1)}, u32[]{:S(2)}) copy-start(bf16[256,256]{1,0:T(8,128)(2,1)} %constant.38.clone.refs_5_) | copy-start | bytes 393220
  21.6 6.0 %copy-start.1 = (bf16[256,256]{1,0:T(8,128)(2,1)S(1)}, bf16[256,256]{1,0:T(8,128)(2,1)}, u32[]{:S(2)}) copy-start(bf16[256,256]{1,0:T(8,128)(2,1)} %constant.37.clone.refs_4_) | copy-start | bytes 393220
  21.6 14.9 %collective-permute-start.6 = (f32[10,32,128]{2,1,0:T(8,128)S(1)}, f32[10,32,128]{2,1,0:T(8,128)S(1)}, u32[]{:S(2)}, u32[]{:S(2)}) collective-permute-start(f32[10,32,128]{2,1,0:T(8,128)S(1)} %get-tuple-element.58), channel_id=1, source_target_pairs={{0,1},{1,0},{2,3},{3,2},{4,5},{5,4},{6,7},{7,6},{8,9},{9,8},{10,11... | collective-permute-start | bytes 491528 | tf_op jit(solution)/shard_map/ppermute | solution.py:260
where the time goes:
time: 37.9 us; the launch traced here: 37.8 us
  starting transfers between devices  15.8 us (42%)
  waiting for transfers between devices  15.3 us (40%)
  Pallas kernels  6.14 us (16%)
    ppermute x6, waiting for transfers between devices, local(): lax.ppermute(blocks[s], 'deep', pairs)  11.8 us
    ppermute x6, starting transfers between devices, local(): lax.ppermute(blocks[s], 'deep', pairs)  8.61 us
    ppermute x6, starting transfers between devices, local(): parts[s] = lax.ppermute(parts[s], 'north', pairs)  7.18 us
    pallas_call x2, Pallas kernels, local(): call(functools.partial(z_kernel, fields, steps_z, deep, start), jax.Shape...  2.43 us
    ppermute x6, waiting for transfers between devices, local(): parts[s] = lax.ppermute(parts[s], 'north', pairs)  2.42 us
    pallas_call x1, Pallas kernels, local(): call(functools.partial(x_kernel, inner, outer, spans), tuple(sends), cost_x)  1.78 us
    ppermute x1, waiting for transfers between devices, local(): taken = hold(lax.ppermute(field, 'north', pairs))  1.08 us
    pallas_call x2, Pallas kernels, local(): call(functools.partial(other_kernel, outer, count, start - first), tuple(...  0.98 us
  transfers between devices with their start and end apart: 13, of which 7 were waited for; matrix products, arithmetic and copies ran while one was open for 1% of the time, Pallas kernels for 11%

commit v1 on v0

--- a/solution.py
+++ b/solution.py
@@ -73,10 +73,16 @@
     )
 
 
-def dot_stacked(a, a_high, b, dims):
-    rows = a_high.shape[0]
-    both = dot(a, b[0], dims)
-    return both[:rows] + (both[rows:] + dot(a_high, b[1], dims))
+def stack_terms(high, low):
+    return jnp.concatenate(
+        [jnp.concatenate([high, high], 1), jnp.concatenate([low, jnp.zeros_like(low)], 1)], 0
+    )
+
+
+def dot_stacked(stacked, columns, dims):
+    rows = stacked.shape[0] // 2
+    both = dot(stacked, columns, dims)
+    return both[:rows] + both[rows:]
 
 
 def x_kernel(inner, outer, chunks, *refs):
@@ -84,10 +90,10 @@
     tables, outs = refs[3 : 3 + len(chunks)], refs[3 + len(chunks) :]
     me = lax.axis_index("north")
     chip, core = me // inner, lax.rem(me, inner)
-    shares = [ref[partner(chip, s, outer), core] for ref in (high, low) for s in range(outer)]
-    table = jnp.concatenate(shares, 0).astype(BF16)
+    shares = [[ref[partner(chip, s, outer), core] for s in range(outer)] for ref in (high, low)]
+    table = stack_terms(*(jnp.concatenate(term, 0).astype(BF16) for term in shares))
     for (first, last, _, _), ref in zip(chunks, tables):
-        ref[...] = jnp.concatenate([rows[first:last] for rows in shares], 0).astype(BF16)
+        ref[...] = stack_terms(*(jnp.concatenate([rows[first:last] for rows in term], 0).astype(BF16) for term in shares))
     for y, s, value in line_modes(field, table, outer):
         for c, (_, _, start, count) in enumerate(chunks):
             outs[c * outer + s][pl.ds(y, count, stride=field.shape[1]), :] = value[start : start + count]
@@ -97,11 +103,10 @@
     fields, lines = field.shape[:2]
     rows = table.shape[0] // 2
     share = rows // outer
-    table_high = table[:rows]
     pair = 2 if lines % 2 == 0 else 1
     for y in range(0, lines, pair):
         columns = jnp.concatenate([field[f, y + i] for i in range(pair) for f in range(fields)], 0)
-        modes = dot_stacked(table, table_high, split(columns), ((1,), (1,)))
+        modes = dot_stacked(table, jnp.concatenate(split(columns), 1), ((1,), (1,)))
         lanes = modes.shape[1] // pair
         for i in range(pair):
             for s in range(outer):
@@ -134,28 +139,28 @@
 
 def y_kernel(inner, outer, deep, order, *refs):
     parts, (high, low), outs = refs[:outer], refs[outer : outer + 2], refs[outer + 2 : outer + 2 + deep]
-    terms = refs[outer + 2 + deep :]
+    terms, total = refs[-1], refs[-1].shape[0] // 2
     me, layer = lax.axis_index("north"), lax.axis_index("deep")
     chip, core = me // inner, lax.rem(me, inner)
     count, share, _ = outs[0].shape
     lines = parts[0].shape[0] // (count * inner)
-    table = jnp.concatenate(
-        [ref[pl.ds(pl.multiple_of(partner(layer, s, deep) * share, share), share), :] for ref in (high, low) for s in range(deep)],
-        0,
-    )
-    table_high = table[: share * deep]
+    table = stack_terms(
+        *(
+            jnp.concatenate([ref[pl.ds(pl.multiple_of(partner(layer, s, deep) * share, share), share), :] for s in range(deep)], 0)
+            for ref in (high, low)
+        )
+    )
     lanes = parts[0].shape[1]
     for r in range(count):
         for part, s in zip(parts, (0, *order)):
             for k in range(inner):
                 at = (source(chip, s, outer) * inner + source(core, k, inner)) * lines
                 at = pl.multiple_of(at, lines)
-                for term, value in zip(terms, split(part[pl.ds((r * inner + k) * lines, lines), :])):
-                    term[pl.ds(at, lines), r * lanes : (r + 1) * lanes] = value
+                for term, value in enumerate(split(part[pl.ds((r * inner + k) * lines, lines), :])):
+                    terms[pl.ds(at + term * total, lines), r * lanes : (r + 1) * lanes] = value
     for r in range(0, count, 2):
         group = range(r, min(r + 2, count))
-        columns = tuple(term[:, r * lanes : (group[-1] + 1) * lanes] for term in terms)
-        modes = dot_stacked(table, table_high, columns, ((1,), (0,)))
+        modes = dot_stacked(table, terms[:, r * lanes : (group[-1] + 1) * lanes], ((1,), (0,)))
         for i in group:
             for s in range(deep):
                 outs[s][i] = modes[s * share : (s + 1) * share, (i - r) * lanes : (i - r + 1) * lanes]
@@ -212,7 +217,7 @@
     for count in chunks:
         spans.append((start // 8 * 8, min(-(-(start + count) // 8) * 8, share_x), start, count))
         start += count
-    sends = [made((2 * outer * (last - first), size_x), BF16) for first, last, _, _ in spans]
+    sends = [made((2 * outer * (last - first), 2 * size_x), BF16) for first, last, _, _ in spans]
     sends += [made((count * lines, lanes)) for count in chunks for _ in range(outer)]
     own = call(functools.partial(x_kernel, inner, outer, spans), tuple(sends), cost_x)(field, *table_x)
     ready_x, own = own[: len(chunks)], own[len(chunks) :]
@@ -235,13 +240,7 @@
                 )(*map(hold, buffers[c]), *map(hold, other))
             buffers[c] = other
 
-    symbol_x, symbol_y, symbol_z, buffers[0] = lax.optimization_barrier((symbol_x, symbol_y, symbol_z, buffers[0]))
-    part_x = lax.dynamic_slice_in_dim(symbol_x, lax.axis_index("north") * share_x, share_x)
-    part_y = lax.dynamic_slice_in_dim(symbol_y, lax.axis_index("deep") * share_y, share_y)
-    symbol = part_x[:, None, None] + part_y[None, :, None] + symbol_z[None, None, :]
-    factor = (1.0 - 0.2 * symbol) / (1.0 + 0.2 * symbol)
-
-    result, start = (), 0
+    received = []
     for c, count in enumerate(chunks):
         north_order = sorted(range(1, outer), key=NORTH_KEY[min(c, 1)])
         parts = list(buffers[c])
@@ -253,11 +252,21 @@
             functools.partial(y_kernel, inner, outer, deep, north_order),
             tuple(made((count, share_y, lanes)) for _ in range(deep)),
             cost_y,
-            scratch=(VMEM((size_y, count * lanes), BF16), VMEM((size_y, count * lanes), BF16)),
+            scratch=(VMEM((2 * size_y, count * lanes), BF16),),
         )(*[hold(parts[s]) for s in (0, *north_order)], *map(hold, table_y))
         sends_z = deep_sends(deep, c)
         steps_z = (0,) + tuple(s for s, _ in sends_z)
         gathered = [blocks[0]] + [lax.ppermute(blocks[s], "deep", pairs) for s, pairs in sends_z]
+        received.append((steps_z, gathered, blocks))
+
+    symbol_x, symbol_y, symbol_z, _ = lax.optimization_barrier((symbol_x, symbol_y, symbol_z, received[-1][2]))
+    part_x = lax.dynamic_slice_in_dim(symbol_x, lax.axis_index("north") * share_x, share_x)
+    part_y = lax.dynamic_slice_in_dim(symbol_y, lax.axis_index("deep") * share_y, share_y)
+    symbol = part_x[:, None, None] + part_y[None, :, None] + symbol_z[None, None, :]
+    factor = (1.0 - 0.2 * symbol) / (1.0 + 0.2 * symbol)
+
+    result, start = (), 0
+    for c, (count, (steps_z, gathered, _)) in enumerate(zip(chunks, received)):
         shape = (fields, share_x, share_y, size_z)
         cost_z = (2 * count * share_y * size_z * size_z * fields * 3, 8 * count * share_y * size_z * fields)
         whole = pl.BlockSpec(memory_space=VMEM)

time: 37.9 us -> 45.5 us (1.20)
  the two profiles are of different devices: /device:TPU:10 before, /device:TPU:12 now
where the time goes in v1:
time: 45.5 us; the launch traced here: 45.3 us
  waiting for transfers between devices  23 us (51%)
  starting transfers between devices  14.5 us (32%)
  Pallas kernels  6.03 us (13%)
  local copies, waits for them, and re-layouts  1.41 us (3%)
    ppermute x6, waiting for transfers between devices, local(): lax.ppermute(blocks[s], 'deep', pairs)  13.5 us
    ppermute x6, waiting for transfers between devices, local(): parts[s] = lax.ppermute(parts[s], 'north', pairs)  8.46 us
    ppermute x6, starting transfers between devices, local(): lax.ppermute(blocks[s], 'deep', pairs)  7.42 us
    ppermute x6, starting transfers between devices, local(): parts[s] = lax.ppermute(parts[s], 'north', pairs)  7.11 us
    pallas_call x2, Pallas kernels, local(): call(functools.partial(z_kernel, fields, steps_z, deep, start), jax.Shape...  2.44 us
    pallas_call x1, Pallas kernels, local(): call(functools.partial(x_kernel, inner, outer, spans), tuple(sends), cost_x)  1.78 us
    unnamed x14, local copies, waits for them, and re-layouts  1.26 us
    ppermute x1, waiting for transfers between devices, local(): taken = hold(lax.ppermute(field, 'north', pairs))  1.08 us
  transfers between devices with their start and end apart: 13, of which 6 were waited for; matrix products, arithmetic and copies ran while one was open for 1% of the time, Pallas kernels for 9%

profile of v1, /device:TPU:12, one launch (start us, length us, event | category | flops | bytes accessed | tf_op | source)
XLA Modules:
  0.0 45.3 jit_solution(13272620091089957621)
XLA Ops:
  0.0 0.0 collective-permute-start
  0.0 1.8 %shard_map.100 = (bf16[64,256]{1,0:T(8,128)(2,1)S(1)}, bf16[128,256]{1,0:T(8,128)(2,1)S(1)}, f32[96,128]{1,0:T(8,128)S(1)}, f32[96,128]{1,0:T(8,128)S(1)}, f32[9...) custom-call(f32[2,16,64,128]{3,2,1,0:T(8,128)} %bitcast.2, ...), custom_call_target="tpu_custom_call" | custom-call | flops 100663296 | bytes 2097152 | tf_op jit(solution)/shard_map/pallas_call | solution.py:222
  1.8 1.1 %collective-permute-done.refs_0_ = f32[2,16,64,128]{3,2,1,0:T(8,128)S(1)} collective-permute-done((f32[2,16,64,128]{3,2,1,0:T(8,128)}, f32[2,16,64,128]{3,2,1,0:T(8,128)S(1)}, u32[]{:S(2)}, u32[]{:S(2)}) %collective-permute-start) | collective-permute-done | bytes 1048608 | tf_op jit(solution)/shard_map/ppermute | solution.py:227
  2.9 0.5 %shard_map.104 = (f32[192,128]{1,0:T(8,128)S(1)}, f32[192,128]{1,0:T(8,128)S(1)}, f32[192,128]{1,0:T(8,128)S(1)}, f32[192,128]{1,0:T(8,128)S(1)}) custom-call(f32[2,16,64,128]{3,2,1,0:T(8,128)S(1)} %collective-permute-done.refs_0_, bf16[64,256]{1,0:T(8,128)(2,1)S(1)} %get-tuple-element.58.refs_1_, f32[96,128]{1,0:T(8,128)S(1)} %get-tuple-element.59.refs_2_, ...), custom_call_target="tpu_custom_call" | custom-call | flops 37748736 | bytes 2097152 | tf_op jit(solution)/shard_map/pallas_call | solution.py:230
  3.3 1.6 %collective-permute-start.7 = (f32[192,128]{1,0:T(8,128)S(1)}, f32[192,128]{1,0:T(8,128)S(1)}, u32[]{:S(2)}, u32[]{:S(2)}) collective-permute-start(f32[192,128]{1,0:T(8,128)S(1)} %get-tuple-element.64), channel_id=1, source_target_pairs={{0,8},{4,12},{8,0},{12,4},{16,24},{20,28},{24,16},{28,20},{1,9},{5... | collective-permute-start | bytes 294920 | tf_op jit(solution)/shard_map/ppermute | solution.py:249
  4.9 0.5 %shard_map.101 = (f32[160,128]{1,0:T(8,128)S(1)}, f32[160,128]{1,0:T(8,128)S(1)}, f32[160,128]{1,0:T(8,128)S(1)}, f32[160,128]{1,0:T(8,128)S(1)}) custom-call(f32[2,16,64,128]{3,2,1,0:T(8,128)S(1)} %collective-permute-done.refs_0_, bf16[128,256]{1,0:T(8,128)(2,1)S(1)} %get-tuple-element.42.refs_1_), custom_call_target="tpu_custom_call" | custom-call | flops 62914560 | bytes 2097152 | tf_op jit(solution)/shard_map/pallas_call | solution.py:230
  5.4 0.0 copy-start.3
  5.5 0.0 copy-start.2
  5.5 0.6 %collective-permute-start.1 = (f32[320,128]{1,0:T(8,128)S(1)}, f32[320,128]{1,0:T(8,128)S(1)}, u32[]{:S(2)}, u32[]{:S(2)}) collective-permute-start(f32[320,128]{1,0:T(8,128)S(1)} %get-tuple-element.48), channel_id=1, source_target_pairs={{0,8},{4,12},{8,0},{12,4},{16,24},{20,28},{24,16},{28,20},{1,9},{5... | collective-permute-start | bytes 491528 | tf_op jit(solution)/shard_map/ppermute | solution.py:249
  6.1 0.5 %collective-permute-start.2 = (f32[320,128]{1,0:T(8,128)S(1)}, f32[320,128]{1,0:T(8,128)S(1)}, u32[]{:S(2)}, u32[]{:S(2)}) collective-permute-start(f32[320,128]{1,0:T(8,128)S(1)} %get-tuple-element.49), channel_id=1, source_target_pairs={{0,16},{4,20},{8,24},{12,28},{16,0},{20,4},{24,8},{28,12},{1,17},{... | collective-permute-start | bytes 491528 | tf_op jit(solution)/shard_map/ppermute | solution.py:249
  6.6 2.4 %collective-permute-start.3 = (f32[320,128]{1,0:T(8,128)S(1)}, f32[320,128]{1,0:T(8,128)S(1)}, u32[]{:S(2)}, u32[]{:S(2)}) collective-permute-start(f32[320,128]{1,0:T(8,128)S(1)} %get-tuple-element.50), channel_id=1, source_target_pairs={{0,24},{4,28},{8,16},{12,20},{16,8},{20,12},{24,0},{28,4},{1,25},{... | collective-permute-start | bytes 491528 | tf_op jit(solution)/shard_map/ppermute | solution.py:249
  9.0 0.5 %collective-permute-start.8 = (f32[192,128]{1,0:T(8,128)S(1)}, f32[192,128]{1,0:T(8,128)S(1)}, u32[]{:S(2)}, u32[]{:S(2)}) collective-permute-start(f32[192,128]{1,0:T(8,128)S(1)} %get-tuple-element.65), channel_id=1, source_target_pairs={{0,16},{4,20},{8,24},{12,28},{16,0},{20,4},{24,8},{28,12},{1,17},{... | collective-permute-start | bytes 294920 | tf_op jit(solution)/shard_map/ppermute | solution.py:249
  9.5 0.0 collective-permute-done.7.refs_1_
  9.5 1.5 %collective-permute-start.9 = (f32[192,128]{1,0:T(8,128)S(1)}, f32[192,128]{1,0:T(8,128)S(1)}, u32[]{:S(2)}, u32[]{:S(2)}) collective-permute-start(f32[192,128]{1,0:T(8,128)S(1)} %get-tuple-element.66), channel_id=1, source_target_pairs={{0,24},{4,28},{8,16},{12,20},{16,8},{20,12},{24,0},{28,4},{1,25},{... | collective-permute-start | bytes 294920 | tf_op jit(solution)/shard_map/ppermute | solution.py:249
  11.0 8.4 %collective-permute-done.8.refs_2_ = f32[192,128]{1,0:T(8,128)S(1)} collective-permute-done((f32[192,128]{1,0:T(8,128)S(1)}, f32[192,128]{1,0:T(8,128)S(1)}, u32[]{:S(2)}, u32[]{:S(2)}) %collective-permute-start.8) | collective-permute-done | bytes 98336 | tf_op jit(solution)/shard_map/ppermute | solution.py:249
  19.5 0.0 collective-permute-done.9.refs_3_
  19.5 0.0 copy-done.3
  19.5 0.0 copy-done.2
  19.5 0.3 shard_map.105
  19.9 1.6 %collective-permute-start.10 = (f32[6,32,128]{2,1,0:T(8,128)S(1)}, f32[6,32,128]{2,1,0:T(8,128)S(1)}, u32[]{:S(2)}, u32[]{:S(2)}) collective-permute-start(f32[6,32,128]{2,1,0:T(8,128)S(1)} %get-tuple-element.68), channel_id=1, source_target_pairs={{0,3},{1,2},{2,1},{3,0},{4,7},{5,6},{6,5},{7,4},{8,11},{9,10},{10,... | collective-permute-start | bytes 294920 | tf_op jit(solution)/shard_map/ppermute | solution.py:259
  21.5 1.2 %collective-permute-start.11 = (f32[6,32,128]{2,1,0:T(8,128)S(1)}, f32[6,32,128]{2,1,0:T(8,128)S(1)}, u32[]{:S(2)}, u32[]{:S(2)}) collective-permute-start(f32[6,32,128]{2,1,0:T(8,128)S(1)} %get-tuple-element.69), channel_id=1, source_target_pairs={{0,2},{1,3},{2,0},{3,1},{4,6},{5,7},{6,4},{7,5},{8,10},{9,11},{10,... | collective-permute-start | bytes 294920 | tf_op jit(solution)/shard_map/ppermute | solution.py:259
  22.7 0.0 collective-permute-done.1.refs_1_
  22.7 1.2 %collective-permute-start.12 = (f32[6,32,128]{2,1,0:T(8,128)S(1)}, f32[6,32,128]{2,1,0:T(8,128)S(1)}, u32[]{:S(2)}, u32[]{:S(2)}) collective-permute-start(f32[6,32,128]{2,1,0:T(8,128)S(1)} %get-tuple-element.70), channel_id=1, source_target_pairs={{0,1},{1,0},{2,3},{3,2},{4,5},{5,4},{6,7},{7,6},{8,9},{9,8},{10,11... | collective-permute-start | bytes 294920 | tf_op jit(solution)/shard_map/ppermute | solution.py:259
  24.0 0.0 collective-permute-done.2.refs_2_
  24.0 0.0 collective-permute-done.3.refs_3_
  24.0 0.5 %shard_map.103 = (f32[10,32,128]{2,1,0:T(8,128)S(1)}, f32[10,32,128]{2,1,0:T(8,128)S(1)}, f32[10,32,128]{2,1,0:T(8,128)S(1)}, f32[10,32,128]{2,1,0:T(8,128)S(1)}) custom-call(f32[320,128]{1,0:T(8,128)S(1)} %get-tuple-element.47.refs_0_, f32[320,128]{1,0:T(8,128)S(1)} %collective-permute-done.1.refs_1_, f32[320,128]{1,0:T(8,128)S(1)} %collective-permute-done.2.refs_2_, ...), custom_call_target="tpu_custom_call" | custom-call | flops 125829120 | bytes 1310720 | tf_op jit(solution)/shard_map/pallas_call | solution.py:251
  24.4 3.0 %collective-permute-start.4 = (f32[10,32,128]{2,1,0:T(8,128)S(1)}, f32[10,32,128]{2,1,0:T(8,128)S(1)}, u32[]{:S(2)}, u32[]{:S(2)}) collective-permute-start(f32[10,32,128]{2,1,0:T(8,128)S(1)} %get-tuple-element.52), channel_id=1, source_target_pairs={{0,2},{1,3},{2,0},{3,1},{4,6},{5,7},{6,4},{7,5},{8,10},{9,11},{10,... | collective-permute-start | bytes 491528 | tf_op jit(solution)/shard_map/ppermute | solution.py:259
  27.4 0.0 collective-permute-start.5
  27.4 0.0 copy-start.5
  27.4 0.7 %copy-done.5 = f32[128]{0:T(128)S(1)} copy-done((f32[128]{0:T(128)S(1)}, f32[128]{0:T(128)}, u32[]{:S(2)}) %copy-start.5) | copy-done | bytes 536
  28.1 0.0 copy-start.6
  28.1 0.1 dynamic_slice.6
  28.2 0.6 %copy-done.6 = f32[128]{0:T(128)S(1)} copy-done((f32[128]{0:T(128)S(1)}, f32[128]{0:T(128)}, u32[]{:S(2)}) %copy-start.6) | copy-done | bytes 536
  28.8 0.1 dynamic_slice.7
  28.8 0.1 broadcast_add_fusion
  28.9 1.3 %collective-permute-done.10.refs_1_ = f32[6,32,128]{2,1,0:T(8,128)S(1)} collective-permute-done((f32[6,32,128]{2,1,0:T(8,128)S(1)}, f32[6,32,128]{2,1,0:T(8,128)S(1)}, u32[]{:S(2)}, u32[]{:S(2)}) %collective-permute-start.10) | collective-permute-done | bytes 98336 | tf_op jit(solution)/shard_map/ppermute | solution.py:259
  30.2 0.3 collective-permute-start.6
  30.5 0.0 copy-done.4
  30.5 0.2 add_divide_fusion.refs_6_
  30.7 6.9 %collective-permute-done.11.refs_2_ = f32[6,32,128]{2,1,0:T(8,128)S(1)} collective-permute-done((f32[6,32,128]{2,1,0:T(8,128)S(1)}, f32[6,32,128]{2,1,0:T(8,128)S(1)}, u32[]{:S(2)}, u32[]{:S(2)}) %collective-permute-start.11) | collective-permute-done | bytes 98336 | tf_op jit(solution)/shard_map/ppermute | solution.py:259
  37.6 0.0 collective-permute-done.12.refs_3_
  37.6 0.0 copy-done
  37.6 0.0 copy-done.1
  37.6 1.1 %shard_map.106.refs_7_ = f32[2,16,32,256]{3,2,1,0:T(8,128)} custom-call(f32[6,32,128]{2,1,0:T(8,128)S(1)} %get-tuple-element.67.refs_0_, f32[6,32,128]{2,1,0:T(8,128)S(1)} %collective-permute-done.10.refs_1_, f32[6,32,128]{2,1,0:T(8,128)S(1)} %collective-permute-done.11.refs_2_, f32[6,32,128]{2,1,0:T(8,128)S(1)} %collective-permute-done.12.refs_3_, ...), custom_call_target="tpu_custom_call" | custom-call | flops 150994944 | bytes 786432 | tf_op jit(solution)/shard_map/pallas_call | solution.py:275
  38.7 2.6 %collective-permute-done.4.refs_1_ = f32[10,32,128]{2,1,0:T(8,128)S(1)} collective-permute-done((f32[10,32,128]{2,1,0:T(8,128)S(1)}, f32[10,32,128]{2,1,0:T(8,128)S(1)}, u32[]{:S(2)}, u32[]{:S(2)}) %collective-permute-start.4) | collective-permute-done | bytes 163872 | tf_op jit(solution)/shard_map/ppermute | solution.py:259
  41.4 2.7 %collective-permute-done.5.refs_2_ = f32[10,32,128]{2,1,0:T(8,128)S(1)} collective-permute-done((f32[10,32,128]{2,1,0:T(8,128)S(1)}, f32[10,32,128]{2,1,0:T(8,128)S(1)}, u32[]{:S(2)}, u32[]{:S(2)}) %collective-permute-start.5) | collective-permute-done | bytes 163872 | tf_op jit(solution)/shard_map/ppermute | solution.py:259
  44.0 0.0 collective-permute-done.6.refs_3_
  44.0 1.3 %shard_map.107 = f32[2,16,32,256]{3,2,1,0:T(8,128)} custom-call(f32[10,32,128]{2,1,0:T(8,128)S(1)} %get-tuple-element.51.refs_0_, f32[10,32,128]{2,1,0:T(8,128)S(1)} %collective-permute-done.4.refs_1_, f32[10,32,128]{2,1,0:T(8,128)S(1)} %collective-permute-done.5.refs_2_, ...), custom_call_target="tpu_custom_call", output_to_operand_aliasing={{}: (7, {})} | custom-call | flops 251658240 | bytes 1310720 | tf_op jit(solution)/shard_map/pallas_call | solution.py:275
  (4 shorter events, 0.1 us)
Async XLA Ops:
  0.0 2.9 %collective-permute-start = (f32[2,16,64,128]{3,2,1,0:T(8,128)}, f32[2,16,64,128]{3,2,1,0:T(8,128)S(1)}, u32[]{:S(2)}, u32[]{:S(2)}) collective-permute-start(f32[2,16,64,128]{3,2,1,0:T(8,128)} %bitcast.1), channel_id=1, source_target_pairs={{0,4},{4,0},{8,12},{12,8},{16,20},{20,16},{24,28},{28,24},{1,5},{5... | collective-permute-start | bytes 3145736 | tf_op jit(solution)/shard_map/ppermute | solution.py:227
  3.3 6.2 %collective-permute-start.7 = (f32[192,128]{1,0:T(8,128)S(1)}, f32[192,128]{1,0:T(8,128)S(1)}, u32[]{:S(2)}, u32[]{:S(2)}) collective-permute-start(f32[192,128]{1,0:T(8,128)S(1)} %get-tuple-element.64), channel_id=1, source_target_pairs={{0,8},{4,12},{8,0},{12,4},{16,24},{20,28},{24,16},{28,20},{1,9},{5... | collective-permute-start | bytes 294920 | tf_op jit(solution)/shard_map/ppermute | solution.py:249
  5.4 14.1 %copy-start.3 = (bf16[128,128]{1,0:T(8,128)(2,1)S(1)}, bf16[128,128]{1,0:T(8,128)(2,1)}, u32[]{:S(2)}) copy-start(bf16[128,128]{1,0:T(8,128)(2,1)} %constant.35.clone.refs_4_) | copy-start | bytes 98308
  5.5 14.0 %copy-start.2 = (bf16[128,128]{1,0:T(8,128)(2,1)S(1)}, bf16[128,128]{1,0:T(8,128)(2,1)}, u32[]{:S(2)}) copy-start(bf16[128,128]{1,0:T(8,128)(2,1)} %constant.36.clone.refs_5_) | copy-start | bytes 98308
  5.5 17.2 %collective-permute-start.1 = (f32[320,128]{1,0:T(8,128)S(1)}, f32[320,128]{1,0:T(8,128)S(1)}, u32[]{:S(2)}, u32[]{:S(2)}) collective-permute-start(f32[320,128]{1,0:T(8,128)S(1)} %get-tuple-element.48), channel_id=1, source_target_pairs={{0,8},{4,12},{8,0},{12,4},{16,24},{20,28},{24,16},{28,20},{1,9},{5... | collective-permute-start | bytes 491528 | tf_op jit(solution)/shard_map/ppermute | solution.py:249
  6.1 17.9 %collective-permute-start.2 = (f32[320,128]{1,0:T(8,128)S(1)}, f32[320,128]{1,0:T(8,128)S(1)}, u32[]{:S(2)}, u32[]{:S(2)}) collective-permute-start(f32[320,128]{1,0:T(8,128)S(1)} %get-tuple-element.49), channel_id=1, source_target_pairs={{0,16},{4,20},{8,24},{12,28},{16,0},{20,4},{24,8},{28,12},{1,17},{... | collective-permute-start | bytes 491528 | tf_op jit(solution)/shard_map/ppermute | solution.py:249
  6.6 17.4 %collective-permute-start.3 = (f32[320,128]{1,0:T(8,128)S(1)}, f32[320,128]{1,0:T(8,128)S(1)}, u32[]{:S(2)}, u32[]{:S(2)}) collective-permute-start(f32[320,128]{1,0:T(8,128)S(1)} %get-tuple-element.50), channel_id=1, source_target_pairs={{0,24},{4,28},{8,16},{12,20},{16,8},{20,12},{24,0},{28,4},{1,25},{... | collective-permute-start | bytes 491528 | tf_op jit(solution)/shard_map/ppermute | solution.py:249
  9.0 10.5 %collective-permute-start.8 = (f32[192,128]{1,0:T(8,128)S(1)}, f32[192,128]{1,0:T(8,128)S(1)}, u32[]{:S(2)}, u32[]{:S(2)}) collective-permute-start(f32[192,128]{1,0:T(8,128)S(1)} %get-tuple-element.65), channel_id=1, source_target_pairs={{0,16},{4,20},{8,24},{12,28},{16,0},{20,4},{24,8},{28,12},{1,17},{... | collective-permute-start | bytes 294920 | tf_op jit(solution)/shard_map/ppermute | solution.py:249
  9.5 9.9 %collective-permute-start.9 = (f32[192,128]{1,0:T(8,128)S(1)}, f32[192,128]{1,0:T(8,128)S(1)}, u32[]{:S(2)}, u32[]{:S(2)}) collective-permute-start(f32[192,128]{1,0:T(8,128)S(1)} %get-tuple-element.66), channel_id=1, source_target_pairs={{0,24},{4,28},{8,16},{12,20},{16,8},{20,12},{24,0},{28,4},{1,25},{... | collective-permute-start | bytes 294920 | tf_op jit(solution)/shard_map/ppermute | solution.py:249
  19.9 10.3 %collective-permute-start.10 = (f32[6,32,128]{2,1,0:T(8,128)S(1)}, f32[6,32,128]{2,1,0:T(8,128)S(1)}, u32[]{:S(2)}, u32[]{:S(2)}) collective-permute-start(f32[6,32,128]{2,1,0:T(8,128)S(1)} %get-tuple-element.68), channel_id=1, source_target_pairs={{0,3},{1,2},{2,1},{3,0},{4,7},{5,6},{6,5},{7,4},{8,11},{9,10},{10,... | collective-permute-start | bytes 294920 | tf_op jit(solution)/shard_map/ppermute | solution.py:259
  21.5 16.1 %collective-permute-start.11 = (f32[6,32,128]{2,1,0:T(8,128)S(1)}, f32[6,32,128]{2,1,0:T(8,128)S(1)}, u32[]{:S(2)}, u32[]{:S(2)}) collective-permute-start(f32[6,32,128]{2,1,0:T(8,128)S(1)} %get-tuple-element.69), channel_id=1, source_target_pairs={{0,2},{1,3},{2,0},{3,1},{4,6},{5,7},{6,4},{7,5},{8,10},{9,11},{10,... | collective-permute-start | bytes 294920 | tf_op jit(solution)/shard_map/ppermute | solution.py:259
  22.7 14.9 %collective-permute-start.12 = (f32[6,32,128]{2,1,0:T(8,128)S(1)}, f32[6,32,128]{2,1,0:T(8,128)S(1)}, u32[]{:S(2)}, u32[]{:S(2)}) collective-permute-start(f32[6,32,128]{2,1,0:T(8,128)S(1)} %get-tuple-element.70), channel_id=1, source_target_pairs={{0,1},{1,0},{2,3},{3,2},{4,5},{5,4},{6,7},{7,6},{8,9},{9,8},{10,11... | collective-permute-start | bytes 294920 | tf_op jit(solution)/shard_map/ppermute | solution.py:259
  24.4 16.9 %collective-permute-start.4 = (f32[10,32,128]{2,1,0:T(8,128)S(1)}, f32[10,32,128]{2,1,0:T(8,128)S(1)}, u32[]{:S(2)}, u32[]{:S(2)}) collective-permute-start(f32[10,32,128]{2,1,0:T(8,128)S(1)} %get-tuple-element.52), channel_id=1, source_target_pairs={{0,2},{1,3},{2,0},{3,1},{4,6},{5,7},{6,4},{7,5},{8,10},{9,11},{10,... | collective-permute-start | bytes 491528 | tf_op jit(solution)/shard_map/ppermute | solution.py:259
  27.4 16.6 %collective-permute-start.5 = (f32[10,32,128]{2,1,0:T(8,128)S(1)}, f32[10,32,128]{2,1,0:T(8,128)S(1)}, u32[]{:S(2)}, u32[]{:S(2)}) collective-permute-start(f32[10,32,128]{2,1,0:T(8,128)S(1)} %get-tuple-element.53), channel_id=1, source_target_pairs={{0,3},{1,2},{2,1},{3,0},{4,7},{5,6},{6,5},{7,4},{8,11},{9,10},{10,... | collective-permute-start | bytes 491528 | tf_op jit(solution)/shard_map/ppermute | solution.py:259
  27.4 0.7 %copy-start.5 = (f32[128]{0:T(128)S(1)}, f32[128]{0:T(128)}, u32[]{:S(2)}) copy-start(f32[128]{0:T(128)} %param.11) | copy-start | bytes 1540
  28.1 0.7 %copy-start.6 = (f32[128]{0:T(128)S(1)}, f32[128]{0:T(128)}, u32[]{:S(2)}) copy-start(f32[128]{0:T(128)} %param.12) | copy-start | bytes 1540
  28.8 1.7 %copy-start.4 = (f32[256]{0:T(256)S(1)}, f32[256]{0:T(256)}, u32[]{:S(2)}) copy-start(f32[256]{0:T(256)} %param.13) | copy-start | bytes 3076
  28.9 8.7 %copy-start = (bf16[256,256]{1,0:T(8,128)(2,1)S(1)}, bf16[256,256]{1,0:T(8,128)(2,1)}, u32[]{:S(2)}) copy-start(bf16[256,256]{1,0:T(8,128)(2,1)} %constant.38.clone.refs_5_) | copy-start | bytes 393220
  28.9 8.7 %copy-start.1 = (bf16[256,256]{1,0:T(8,128)(2,1)S(1)}, bf16[256,256]{1,0:T(8,128)(2,1)}, u32[]{:S(2)}) copy-start(bf16[256,256]{1,0:T(8,128)(2,1)} %constant.37.clone.refs_4_) | copy-start | bytes 393220
  30.2 13.8 %collective-permute-start.6 = (f32[10,32,128]{2,1,0:T(8,128)S(1)}, f32[10,32,128]{2,1,0:T(8,128)S(1)}, u32[]{:S(2)}, u32[]{:S(2)}) collective-permute-start(f32[10,32,128]{2,1,0:T(8,128)S(1)} %get-tuple-element.54), channel_id=1, source_target_pairs={{0,1},{1,0},{2,3},{3,2},{4,5},{5,4},{6,7},{7,6},{8,9},{9,8},{10,11... | collective-permute-start | bytes 491528 | tf_op jit(solution)/shard_map/ppermute | solution.py:259

commit v2 on v1

--- a/solution.py
+++ b/solution.py
@@ -36,6 +36,7 @@
     return dot(a[0], b[0], dims) + (dot(a[0], b[1], dims) + dot(a[1], b[0], dims))
 
 
+CUTS = 2
 NORTH_KEY = (lambda s: s, lambda s: s)
 NEAR_BYTES = 2**20
 
@@ -185,11 +186,16 @@
         lines = tuple(
             jnp.concatenate([piece[term][:, f * depth : (f + 1) * depth] for piece in pieces], 1) for term in range(2)
         )
-        modes = dot3(lines, table, ((1,), (0,)))
-        stage[f] = modes.reshape(count, modes_y, modes.shape[1]) * factor[start : start + count]
-        copy = pltpu.make_async_copy(stage.at[f], out.at[f, pl.ds(start, count)], sems.at[f])
-        copy.start()
-        copies.append(copy)
+        for i in range(CUTS):
+            first, last = count * i // CUTS, count * (i + 1) // CUTS
+            part = tuple(term[first * modes_y : last * modes_y] for term in lines)
+            modes = dot3(part, table, ((1,), (0,)))
+            stage[f, first:last] = modes.reshape(last - first, modes_y, modes.shape[1]) * factor[start + first : start + last]
+            copy = pltpu.make_async_copy(
+                stage.at[f, pl.ds(first, last - first)], out.at[f, pl.ds(start + first, last - first)], sems.at[f, i]
+            )
+            copy.start()
+            copies.append(copy)
     for copy in copies:
         copy.wait()
 
@@ -277,7 +283,7 @@
                 jax.ShapeDtypeStruct(shape, F32),
                 cost_z,
                 aliases={len(steps_z) + 3: 0} if c else {},
-                scratch=(VMEM((fields, count) + shape[2:], F32), pltpu.SemaphoreType.DMA((fields,))),
+                scratch=(VMEM((fields, count) + shape[2:], F32), pltpu.SemaphoreType.DMA((fields, CUTS))),
                 in_specs=[whole] * (len(steps_z) + 3) + [anywhere] * len(result),
                 out_specs=anywhere,
             )(*map(hold, gathered), *map(hold, table_z), hold(factor), *result),

time: 45.5 us -> 45.4 us (level)
  no operation moved by 1% of the time
where the time goes in v2:
time: 45.4 us; the launch traced here: 45.3 us
  waiting for transfers between devices  23 us (51%)
  starting transfers between devices  14.5 us (32%)
  Pallas kernels  5.95 us (13%)
  local copies, waits for them, and re-layouts  1.41 us (3%)
    ppermute x6, waiting for transfers between devices, local(): lax.ppermute(blocks[s], 'deep', pairs)  13.5 us
    ppermute x6, waiting for transfers between devices, local(): parts[s] = lax.ppermute(parts[s], 'north', pairs)  8.46 us
    ppermute x6, starting transfers between devices, local(): lax.ppermute(blocks[s], 'deep', pairs)  7.42 us
    ppermute x6, starting transfers between devices, local(): parts[s] = lax.ppermute(parts[s], 'north', pairs)  7.11 us
    pallas_call x2, Pallas kernels, local(): call(functools.partial(z_kernel, fields, steps_z, deep, start), jax.Shape...  2.36 us
    pallas_call x1, Pallas kernels, local(): call(functools.partial(x_kernel, inner, outer, spans), tuple(sends), cost_x)  1.78 us
    unnamed x14, local copies, waits for them, and re-layouts  1.26 us
    ppermute x1, waiting for transfers between devices, local(): taken = hold(lax.ppermute(field, 'north', pairs))  1.08 us
  transfers between devices with their start and end apart: 13, of which 6 were waited for; matrix products, arithmetic and copies ran while one was open for 1% of the time, Pallas kernels for 9%

profile of v2, /device:TPU:12, one launch (start us, length us, event | category | flops | bytes accessed | tf_op | source)
XLA Modules:
  0.0 45.3 jit_solution(10905855599907987939)
XLA Ops:
  0.0 0.0 collective-permute-start
  0.0 1.8 %shard_map.100 = (bf16[64,256]{1,0:T(8,128)(2,1)S(1)}, bf16[128,256]{1,0:T(8,128)(2,1)S(1)}, f32[96,128]{1,0:T(8,128)S(1)}, f32[96,128]{1,0:T(8,128)S(1)}, f32[9...) custom-call(f32[2,16,64,128]{3,2,1,0:T(8,128)} %bitcast.2, ...), custom_call_target="tpu_custom_call" | custom-call | flops 100663296 | bytes 2097152 | tf_op jit(solution)/shard_map/pallas_call | solution.py:228
  1.8 1.1 %collective-permute-done.refs_0_ = f32[2,16,64,128]{3,2,1,0:T(8,128)S(1)} collective-permute-done((f32[2,16,64,128]{3,2,1,0:T(8,128)}, f32[2,16,64,128]{3,2,1,0:T(8,128)S(1)}, u32[]{:S(2)}, u32[]{:S(2)}) %collective-permute-start) | collective-permute-done | bytes 1048608 | tf_op jit(solution)/shard_map/ppermute | solution.py:233
  2.9 0.5 %shard_map.104 = (f32[192,128]{1,0:T(8,128)S(1)}, f32[192,128]{1,0:T(8,128)S(1)}, f32[192,128]{1,0:T(8,128)S(1)}, f32[192,128]{1,0:T(8,128)S(1)}) custom-call(f32[2,16,64,128]{3,2,1,0:T(8,128)S(1)} %collective-permute-done.refs_0_, bf16[64,256]{1,0:T(8,128)(2,1)S(1)} %get-tuple-element.58.refs_1_, f32[96,128]{1,0:T(8,128)S(1)} %get-tuple-element.59.refs_2_, ...), custom_call_target="tpu_custom_call" | custom-call | flops 37748736 | bytes 2097152 | tf_op jit(solution)/shard_map/pallas_call | solution.py:236
  3.3 1.6 %collective-permute-start.7 = (f32[192,128]{1,0:T(8,128)S(1)}, f32[192,128]{1,0:T(8,128)S(1)}, u32[]{:S(2)}, u32[]{:S(2)}) collective-permute-start(f32[192,128]{1,0:T(8,128)S(1)} %get-tuple-element.64), channel_id=1, source_target_pairs={{0,8},{4,12},{8,0},{12,4},{16,24},{20,28},{24,16},{28,20},{1,9},{5... | collective-permute-start | bytes 294920 | tf_op jit(solution)/shard_map/ppermute | solution.py:255
  4.9 0.5 %shard_map.101 = (f32[160,128]{1,0:T(8,128)S(1)}, f32[160,128]{1,0:T(8,128)S(1)}, f32[160,128]{1,0:T(8,128)S(1)}, f32[160,128]{1,0:T(8,128)S(1)}) custom-call(f32[2,16,64,128]{3,2,1,0:T(8,128)S(1)} %collective-permute-done.refs_0_, bf16[128,256]{1,0:T(8,128)(2,1)S(1)} %get-tuple-element.42.refs_1_), custom_call_target="tpu_custom_call" | custom-call | flops 62914560 | bytes 2097152 | tf_op jit(solution)/shard_map/pallas_call | solution.py:236
  5.4 0.0 copy-start.3
  5.5 0.0 copy-start.2
  5.5 0.6 %collective-permute-start.1 = (f32[320,128]{1,0:T(8,128)S(1)}, f32[320,128]{1,0:T(8,128)S(1)}, u32[]{:S(2)}, u32[]{:S(2)}) collective-permute-start(f32[320,128]{1,0:T(8,128)S(1)} %get-tuple-element.48), channel_id=1, source_target_pairs={{0,8},{4,12},{8,0},{12,4},{16,24},{20,28},{24,16},{28,20},{1,9},{5... | collective-permute-start | bytes 491528 | tf_op jit(solution)/shard_map/ppermute | solution.py:255
  6.1 0.5 %collective-permute-start.2 = (f32[320,128]{1,0:T(8,128)S(1)}, f32[320,128]{1,0:T(8,128)S(1)}, u32[]{:S(2)}, u32[]{:S(2)}) collective-permute-start(f32[320,128]{1,0:T(8,128)S(1)} %get-tuple-element.49), channel_id=1, source_target_pairs={{0,16},{4,20},{8,24},{12,28},{16,0},{20,4},{24,8},{28,12},{1,17},{... | collective-permute-start | bytes 491528 | tf_op jit(solution)/shard_map/ppermute | solution.py:255
  6.6 2.4 %collective-permute-start.3 = (f32[320,128]{1,0:T(8,128)S(1)}, f32[320,128]{1,0:T(8,128)S(1)}, u32[]{:S(2)}, u32[]{:S(2)}) collective-permute-start(f32[320,128]{1,0:T(8,128)S(1)} %get-tuple-element.50), channel_id=1, source_target_pairs={{0,24},{4,28},{8,16},{12,20},{16,8},{20,12},{24,0},{28,4},{1,25},{... | collective-permute-start | bytes 491528 | tf_op jit(solution)/shard_map/ppermute | solution.py:255
  9.0 0.5 %collective-permute-start.8 = (f32[192,128]{1,0:T(8,128)S(1)}, f32[192,128]{1,0:T(8,128)S(1)}, u32[]{:S(2)}, u32[]{:S(2)}) collective-permute-start(f32[192,128]{1,0:T(8,128)S(1)} %get-tuple-element.65), channel_id=1, source_target_pairs={{0,16},{4,20},{8,24},{12,28},{16,0},{20,4},{24,8},{28,12},{1,17},{... | collective-permute-start | bytes 294920 | tf_op jit(solution)/shard_map/ppermute | solution.py:255
  9.5 0.0 collective-permute-done.7.refs_1_
  9.5 1.5 %collective-permute-start.9 = (f32[192,128]{1,0:T(8,128)S(1)}, f32[192,128]{1,0:T(8,128)S(1)}, u32[]{:S(2)}, u32[]{:S(2)}) collective-permute-start(f32[192,128]{1,0:T(8,128)S(1)} %get-tuple-element.66), channel_id=1, source_target_pairs={{0,24},{4,28},{8,16},{12,20},{16,8},{20,12},{24,0},{28,4},{1,25},{... | collective-permute-start | bytes 294920 | tf_op jit(solution)/shard_map/ppermute | solution.py:255
  11.0 8.4 %collective-permute-done.8.refs_2_ = f32[192,128]{1,0:T(8,128)S(1)} collective-permute-done((f32[192,128]{1,0:T(8,128)S(1)}, f32[192,128]{1,0:T(8,128)S(1)}, u32[]{:S(2)}, u32[]{:S(2)}) %collective-permute-start.8) | collective-permute-done | bytes 98336 | tf_op jit(solution)/shard_map/ppermute | solution.py:255
  19.5 0.0 collective-permute-done.9.refs_3_
  19.5 0.0 copy-done.3
  19.5 0.0 copy-done.2
  19.5 0.3 shard_map.105
  19.9 1.6 %collective-permute-start.10 = (f32[6,32,128]{2,1,0:T(8,128)S(1)}, f32[6,32,128]{2,1,0:T(8,128)S(1)}, u32[]{:S(2)}, u32[]{:S(2)}) collective-permute-start(f32[6,32,128]{2,1,0:T(8,128)S(1)} %get-tuple-element.68), channel_id=1, source_target_pairs={{0,3},{1,2},{2,1},{3,0},{4,7},{5,6},{6,5},{7,4},{8,11},{9,10},{10,... | collective-permute-start | bytes 294920 | tf_op jit(solution)/shard_map/ppermute | solution.py:265
  21.5 1.2 %collective-permute-start.11 = (f32[6,32,128]{2,1,0:T(8,128)S(1)}, f32[6,32,128]{2,1,0:T(8,128)S(1)}, u32[]{:S(2)}, u32[]{:S(2)}) collective-permute-start(f32[6,32,128]{2,1,0:T(8,128)S(1)} %get-tuple-element.69), channel_id=1, source_target_pairs={{0,2},{1,3},{2,0},{3,1},{4,6},{5,7},{6,4},{7,5},{8,10},{9,11},{10,... | collective-permute-start | bytes 294920 | tf_op jit(solution)/shard_map/ppermute | solution.py:265
  22.7 0.0 collective-permute-done.1.refs_1_
  22.7 1.2 %collective-permute-start.12 = (f32[6,32,128]{2,1,0:T(8,128)S(1)}, f32[6,32,128]{2,1,0:T(8,128)S(1)}, u32[]{:S(2)}, u32[]{:S(2)}) collective-permute-start(f32[6,32,128]{2,1,0:T(8,128)S(1)} %get-tuple-element.70), channel_id=1, source_target_pairs={{0,1},{1,0},{2,3},{3,2},{4,5},{5,4},{6,7},{7,6},{8,9},{9,8},{10,11... | collective-permute-start | bytes 294920 | tf_op jit(solution)/shard_map/ppermute | solution.py:265
  24.0 0.0 collective-permute-done.2.refs_2_
  24.0 0.0 collective-permute-done.3.refs_3_
  24.0 0.5 %shard_map.103 = (f32[10,32,128]{2,1,0:T(8,128)S(1)}, f32[10,32,128]{2,1,0:T(8,128)S(1)}, f32[10,32,128]{2,1,0:T(8,128)S(1)}, f32[10,32,128]{2,1,0:T(8,128)S(1)}) custom-call(f32[320,128]{1,0:T(8,128)S(1)} %get-tuple-element.47.refs_0_, f32[320,128]{1,0:T(8,128)S(1)} %collective-permute-done.1.refs_1_, f32[320,128]{1,0:T(8,128)S(1)} %collective-permute-done.2.refs_2_, ...), custom_call_target="tpu_custom_call" | custom-call | flops 125829120 | bytes 1310720 | tf_op jit(solution)/shard_map/pallas_call | solution.py:257
  24.4 3.0 %collective-permute-start.4 = (f32[10,32,128]{2,1,0:T(8,128)S(1)}, f32[10,32,128]{2,1,0:T(8,128)S(1)}, u32[]{:S(2)}, u32[]{:S(2)}) collective-permute-start(f32[10,32,128]{2,1,0:T(8,128)S(1)} %get-tuple-element.52), channel_id=1, source_target_pairs={{0,2},{1,3},{2,0},{3,1},{4,6},{5,7},{6,4},{7,5},{8,10},{9,11},{10,... | collective-permute-start | bytes 491528 | tf_op jit(solution)/shard_map/ppermute | solution.py:265
  27.4 0.0 collective-permute-start.5
  27.4 0.0 copy-start.5
  27.4 0.7 %copy-done.5 = f32[128]{0:T(128)S(1)} copy-done((f32[128]{0:T(128)S(1)}, f32[128]{0:T(128)}, u32[]{:S(2)}) %copy-start.5) | copy-done | bytes 536
  28.1 0.0 copy-start.6
  28.1 0.1 dynamic_slice.6
  28.2 0.6 %copy-done.6 = f32[128]{0:T(128)S(1)} copy-done((f32[128]{0:T(128)S(1)}, f32[128]{0:T(128)}, u32[]{:S(2)}) %copy-start.6) | copy-done | bytes 536
  28.8 0.1 dynamic_slice.7
  28.8 0.1 broadcast_add_fusion
  28.9 1.3 %collective-permute-done.10.refs_1_ = f32[6,32,128]{2,1,0:T(8,128)S(1)} collective-permute-done((f32[6,32,128]{2,1,0:T(8,128)S(1)}, f32[6,32,128]{2,1,0:T(8,128)S(1)}, u32[]{:S(2)}, u32[]{:S(2)}) %collective-permute-start.10) | collective-permute-done | bytes 98336 | tf_op jit(solution)/shard_map/ppermute | solution.py:265
  30.2 0.3 collective-permute-start.6
  30.5 0.0 copy-done.4
  30.5 0.2 add_divide_fusion.refs_6_
  30.7 6.9 %collective-permute-done.11.refs_2_ = f32[6,32,128]{2,1,0:T(8,128)S(1)} collective-permute-done((f32[6,32,128]{2,1,0:T(8,128)S(1)}, f32[6,32,128]{2,1,0:T(8,128)S(1)}, u32[]{:S(2)}, u32[]{:S(2)}) %collective-permute-start.11) | collective-permute-done | bytes 98336 | tf_op jit(solution)/shard_map/ppermute | solution.py:265
  37.6 0.0 collective-permute-done.12.refs_3_
  37.6 0.0 copy-done
  37.6 0.0 copy-done.1
  37.6 1.1 %shard_map.106.refs_7_ = f32[2,16,32,256]{3,2,1,0:T(8,128)} custom-call(f32[6,32,128]{2,1,0:T(8,128)S(1)} %get-tuple-element.67.refs_0_, f32[6,32,128]{2,1,0:T(8,128)S(1)} %collective-permute-done.10.refs_1_, f32[6,32,128]{2,1,0:T(8,128)S(1)} %collective-permute-done.11.refs_2_, f32[6,32,128]{2,1,0:T(8,128)S(1)} %collective-permute-done.12.refs_3_, ...), custom_call_target="tpu_custom_call" | custom-call | flops 150994944 | bytes 786432 | tf_op jit(solution)/shard_map/pallas_call | solution.py:281
  38.7 2.6 %collective-permute-done.4.refs_1_ = f32[10,32,128]{2,1,0:T(8,128)S(1)} collective-permute-done((f32[10,32,128]{2,1,0:T(8,128)S(1)}, f32[10,32,128]{2,1,0:T(8,128)S(1)}, u32[]{:S(2)}, u32[]{:S(2)}) %collective-permute-start.4) | collective-permute-done | bytes 163872 | tf_op jit(solution)/shard_map/ppermute | solution.py:265
  41.4 2.7 %collective-permute-done.5.refs_2_ = f32[10,32,128]{2,1,0:T(8,128)S(1)} collective-permute-done((f32[10,32,128]{2,1,0:T(8,128)S(1)}, f32[10,32,128]{2,1,0:T(8,128)S(1)}, u32[]{:S(2)}, u32[]{:S(2)}) %collective-permute-start.5) | collective-permute-done | bytes 163872 | tf_op jit(solution)/shard_map/ppermute | solution.py:265
  44.0 0.0 collective-permute-done.6.refs_3_
  44.0 1.2 %shard_map.107 = f32[2,16,32,256]{3,2,1,0:T(8,128)} custom-call(f32[10,32,128]{2,1,0:T(8,128)S(1)} %get-tuple-element.51.refs_0_, f32[10,32,128]{2,1,0:T(8,128)S(1)} %collective-permute-done.4.refs_1_, f32[10,32,128]{2,1,0:T(8,128)S(1)} %collective-permute-done.5.refs_2_, ...), custom_call_target="tpu_custom_call", output_to_operand_aliasing={{}: (7, {})} | custom-call | flops 251658240 | bytes 1310720 | tf_op jit(solution)/shard_map/pallas_call | solution.py:281
  (4 shorter events, 0.1 us)
Async XLA Ops:
  0.0 2.9 %collective-permute-start = (f32[2,16,64,128]{3,2,1,0:T(8,128)}, f32[2,16,64,128]{3,2,1,0:T(8,128)S(1)}, u32[]{:S(2)}, u32[]{:S(2)}) collective-permute-start(f32[2,16,64,128]{3,2,1,0:T(8,128)} %bitcast.1), channel_id=1, source_target_pairs={{0,4},{4,0},{8,12},{12,8},{16,20},{20,16},{24,28},{28,24},{1,5},{5... | collective-permute-start | bytes 3145736 | tf_op jit(solution)/shard_map/ppermute | solution.py:233
  3.3 6.2 %collective-permute-start.7 = (f32[192,128]{1,0:T(8,128)S(1)}, f32[192,128]{1,0:T(8,128)S(1)}, u32[]{:S(2)}, u32[]{:S(2)}) collective-permute-start(f32[192,128]{1,0:T(8,128)S(1)} %get-tuple-element.64), channel_id=1, source_target_pairs={{0,8},{4,12},{8,0},{12,4},{16,24},{20,28},{24,16},{28,20},{1,9},{5... | collective-permute-start | bytes 294920 | tf_op jit(solution)/shard_map/ppermute | solution.py:255
  5.4 14.1 %copy-start.3 = (bf16[128,128]{1,0:T(8,128)(2,1)S(1)}, bf16[128,128]{1,0:T(8,128)(2,1)}, u32[]{:S(2)}) copy-start(bf16[128,128]{1,0:T(8,128)(2,1)} %constant.35.clone.refs_4_) | copy-start | bytes 98308
  5.5 14.0 %copy-start.2 = (bf16[128,128]{1,0:T(8,128)(2,1)S(1)}, bf16[128,128]{1,0:T(8,128)(2,1)}, u32[]{:S(2)}) copy-start(bf16[128,128]{1,0:T(8,128)(2,1)} %constant.36.clone.refs_5_) | copy-start | bytes 98308
  5.5 17.2 %collective-permute-start.1 = (f32[320,128]{1,0:T(8,128)S(1)}, f32[320,128]{1,0:T(8,128)S(1)}, u32[]{:S(2)}, u32[]{:S(2)}) collective-permute-start(f32[320,128]{1,0:T(8,128)S(1)} %get-tuple-element.48), channel_id=1, source_target_pairs={{0,8},{4,12},{8,0},{12,4},{16,24},{20,28},{24,16},{28,20},{1,9},{5... | collective-permute-start | bytes 491528 | tf_op jit(solution)/shard_map/ppermute | solution.py:255
  6.1 17.9 %collective-permute-start.2 = (f32[320,128]{1,0:T(8,128)S(1)}, f32[320,128]{1,0:T(8,128)S(1)}, u32[]{:S(2)}, u32[]{:S(2)}) collective-permute-start(f32[320,128]{1,0:T(8,128)S(1)} %get-tuple-element.49), channel_id=1, source_target_pairs={{0,16},{4,20},{8,24},{12,28},{16,0},{20,4},{24,8},{28,12},{1,17},{... | collective-permute-start | bytes 491528 | tf_op jit(solution)/shard_map/ppermute | solution.py:255
  6.6 17.4 %collective-permute-start.3 = (f32[320,128]{1,0:T(8,128)S(1)}, f32[320,128]{1,0:T(8,128)S(1)}, u32[]{:S(2)}, u32[]{:S(2)}) collective-permute-start(f32[320,128]{1,0:T(8,128)S(1)} %get-tuple-element.50), channel_id=1, source_target_pairs={{0,24},{4,28},{8,16},{12,20},{16,8},{20,12},{24,0},{28,4},{1,25},{... | collective-permute-start | bytes 491528 | tf_op jit(solution)/shard_map/ppermute | solution.py:255
  9.0 10.5 %collective-permute-start.8 = (f32[192,128]{1,0:T(8,128)S(1)}, f32[192,128]{1,0:T(8,128)S(1)}, u32[]{:S(2)}, u32[]{:S(2)}) collective-permute-start(f32[192,128]{1,0:T(8,128)S(1)} %get-tuple-element.65), channel_id=1, source_target_pairs={{0,16},{4,20},{8,24},{12,28},{16,0},{20,4},{24,8},{28,12},{1,17},{... | collective-permute-start | bytes 294920 | tf_op jit(solution)/shard_map/ppermute | solution.py:255
  9.5 9.9 %collective-permute-start.9 = (f32[192,128]{1,0:T(8,128)S(1)}, f32[192,128]{1,0:T(8,128)S(1)}, u32[]{:S(2)}, u32[]{:S(2)}) collective-permute-start(f32[192,128]{1,0:T(8,128)S(1)} %get-tuple-element.66), channel_id=1, source_target_pairs={{0,24},{4,28},{8,16},{12,20},{16,8},{20,12},{24,0},{28,4},{1,25},{... | collective-permute-start | bytes 294920 | tf_op jit(solution)/shard_map/ppermute | solution.py:255
  19.9 10.3 %collective-permute-start.10 = (f32[6,32,128]{2,1,0:T(8,128)S(1)}, f32[6,32,128]{2,1,0:T(8,128)S(1)}, u32[]{:S(2)}, u32[]{:S(2)}) collective-permute-start(f32[6,32,128]{2,1,0:T(8,128)S(1)} %get-tuple-element.68), channel_id=1, source_target_pairs={{0,3},{1,2},{2,1},{3,0},{4,7},{5,6},{6,5},{7,4},{8,11},{9,10},{10,... | collective-permute-start | bytes 294920 | tf_op jit(solution)/shard_map/ppermute | solution.py:265
  21.5 16.1 %collective-permute-start.11 = (f32[6,32,128]{2,1,0:T(8,128)S(1)}, f32[6,32,128]{2,1,0:T(8,128)S(1)}, u32[]{:S(2)}, u32[]{:S(2)}) collective-permute-start(f32[6,32,128]{2,1,0:T(8,128)S(1)} %get-tuple-element.69), channel_id=1, source_target_pairs={{0,2},{1,3},{2,0},{3,1},{4,6},{5,7},{6,4},{7,5},{8,10},{9,11},{10,... | collective-permute-start | bytes 294920 | tf_op jit(solution)/shard_map/ppermute | solution.py:265
  22.7 14.9 %collective-permute-start.12 = (f32[6,32,128]{2,1,0:T(8,128)S(1)}, f32[6,32,128]{2,1,0:T(8,128)S(1)}, u32[]{:S(2)}, u32[]{:S(2)}) collective-permute-start(f32[6,32,128]{2,1,0:T(8,128)S(1)} %get-tuple-element.70), channel_id=1, source_target_pairs={{0,1},{1,0},{2,3},{3,2},{4,5},{5,4},{6,7},{7,6},{8,9},{9,8},{10,11... | collective-permute-start | bytes 294920 | tf_op jit(solution)/shard_map/ppermute | solution.py:265
  24.4 16.9 %collective-permute-start.4 = (f32[10,32,128]{2,1,0:T(8,128)S(1)}, f32[10,32,128]{2,1,0:T(8,128)S(1)}, u32[]{:S(2)}, u32[]{:S(2)}) collective-permute-start(f32[10,32,128]{2,1,0:T(8,128)S(1)} %get-tuple-element.52), channel_id=1, source_target_pairs={{0,2},{1,3},{2,0},{3,1},{4,6},{5,7},{6,4},{7,5},{8,10},{9,11},{10,... | collective-permute-start | bytes 491528 | tf_op jit(solution)/shard_map/ppermute | solution.py:265
  27.4 16.6 %collective-permute-start.5 = (f32[10,32,128]{2,1,0:T(8,128)S(1)}, f32[10,32,128]{2,1,0:T(8,128)S(1)}, u32[]{:S(2)}, u32[]{:S(2)}) collective-permute-start(f32[10,32,128]{2,1,0:T(8,128)S(1)} %get-tuple-element.53), channel_id=1, source_target_pairs={{0,3},{1,2},{2,1},{3,0},{4,7},{5,6},{6,5},{7,4},{8,11},{9,10},{10,... | collective-permute-start | bytes 491528 | tf_op jit(solution)/shard_map/ppermute | solution.py:265
  27.4 0.7 %copy-start.5 = (f32[128]{0:T(128)S(1)}, f32[128]{0:T(128)}, u32[]{:S(2)}) copy-start(f32[128]{0:T(128)} %param.11) | copy-start | bytes 1540
  28.1 0.7 %copy-start.6 = (f32[128]{0:T(128)S(1)}, f32[128]{0:T(128)}, u32[]{:S(2)}) copy-start(f32[128]{0:T(128)} %param.12) | copy-start | bytes 1540
  28.8 1.7 %copy-start.4 = (f32[256]{0:T(256)S(1)}, f32[256]{0:T(256)}, u32[]{:S(2)}) copy-start(f32[256]{0:T(256)} %param.13) | copy-start | bytes 3076
  28.9 8.7 %copy-start = (bf16[256,256]{1,0:T(8,128)(2,1)S(1)}, bf16[256,256]{1,0:T(8,128)(2,1)}, u32[]{:S(2)}) copy-start(bf16[256,256]{1,0:T(8,128)(2,1)} %constant.38.clone.refs_5_) | copy-start | bytes 393220
  28.9 8.7 %copy-start.1 = (bf16[256,256]{1,0:T(8,128)(2,1)S(1)}, bf16[256,256]{1,0:T(8,128)(2,1)}, u32[]{:S(2)}) copy-start(bf16[256,256]{1,0:T(8,128)(2,1)} %constant.37.clone.refs_4_) | copy-start | bytes 393220
  30.2 13.8 %collective-permute-start.6 = (f32[10,32,128]{2,1,0:T(8,128)S(1)}, f32[10,32,128]{2,1,0:T(8,128)S(1)}, u32[]{:S(2)}, u32[]{:S(2)}) collective-permute-start(f32[10,32,128]{2,1,0:T(8,128)S(1)} %get-tuple-element.54), channel_id=1, source_target_pairs={{0,1},{1,0},{2,3},{3,2},{4,5},{5,4},{6,7},{7,6},{8,9},{9,8},{10,11... | collective-permute-start | bytes 491528 | tf_op jit(solution)/shard_map/ppermute | solution.py:265

commit v3 on v2

--- a/solution.py
+++ b/solution.py
@@ -86,9 +86,10 @@
     return both[:rows] + both[rows:]
 
 
-def x_kernel(inner, outer, chunks, *refs):
+def x_kernel(inner, outer, deep, chunks, *refs):
     field, high, low = refs[:3]
-    tables, outs = refs[3 : 3 + len(chunks)], refs[3 + len(chunks) :]
+    tables, outs = refs[5 : 5 + len(chunks)], refs[5 + len(chunks) : -1]
+    refs[-1][...] = y_table(deep, refs[3:5])
     me = lax.axis_index("north")
     chip, core = me // inner, lax.rem(me, inner)
     shares = [[ref[partner(chip, s, outer), core] for s in range(outer)] for ref in (high, low)]
@@ -138,19 +139,23 @@
     join(count, (refs[:outer], refs[outer : 2 * outer]), refs[2 * outer :])
 
 
+def y_table(deep, terms):
+    layer, share = lax.axis_index("deep"), terms[0].shape[0] // deep
+    return stack_terms(
+        *(
+            jnp.concatenate([ref[pl.ds(pl.multiple_of(partner(layer, s, deep) * share, share), share), :] for s in range(deep)], 0)
+            for ref in terms
+        )
+    )
+
+
 def y_kernel(inner, outer, deep, order, *refs):
-    parts, (high, low), outs = refs[:outer], refs[outer : outer + 2], refs[outer + 2 : outer + 2 + deep]
+    parts, table, outs = refs[:outer], refs[outer][...], refs[outer + 1 : outer + 1 + deep]
     terms, total = refs[-1], refs[-1].shape[0] // 2
-    me, layer = lax.axis_index("north"), lax.axis_index("deep")
+    me = lax.axis_index("north")
     chip, core = me // inner, lax.rem(me, inner)
     count, share, _ = outs[0].shape
     lines = parts[0].shape[0] // (count * inner)
-    table = stack_terms(
-        *(
-            jnp.concatenate([ref[pl.ds(pl.multiple_of(partner(layer, s, deep) * share, share), share), :] for s in range(deep)], 0)
-            for ref in (high, low)
-        )
-    )
     lanes = parts[0].shape[1]
     for r in range(count):
         for part, s in zip(parts, (0, *order)):
@@ -167,6 +172,10 @@
                 outs[s][i] = modes[s * share : (s + 1) * share, (i - r) * lanes : (i - r + 1) * lanes]
 
 
+def cut_at(count, i):
+    return (0, count * 3 // 5, count)[i]
+
+
 def z_kernel(fields, steps, deep, start, *refs):
     high, low, factor = refs[len(steps) : len(steps) + 3]
     out, stage, sems = refs[-3:]
@@ -187,7 +196,7 @@
             jnp.concatenate([piece[term][:, f * depth : (f + 1) * depth] for piece in pieces], 1) for term in range(2)
         )
         for i in range(CUTS):
-            first, last = count * i // CUTS, count * (i + 1) // CUTS
+            first, last = cut_at(count, i), cut_at(count, i + 1)
             part = tuple(term[first * modes_y : last * modes_y] for term in lines)
             modes = dot3(part, table, ((1,), (0,)))
             stage[f, first:last] = modes.reshape(last - first, modes_y, modes.shape[1]) * factor[start + first : start + last]
@@ -225,7 +234,8 @@
         start += count
     sends = [made((2 * outer * (last - first), 2 * size_x), BF16) for first, last, _, _ in spans]
     sends += [made((count * lines, lanes)) for count in chunks for _ in range(outer)]
-    own = call(functools.partial(x_kernel, inner, outer, spans), tuple(sends), cost_x)(field, *table_x)
+    sends.append(made((2 * size_y, 2 * size_y), BF16))
+    *own, ready_y = call(functools.partial(x_kernel, inner, outer, deep, spans), tuple(sends), cost_x)(field, *table_x, *table_y)
     ready_x, own = own[: len(chunks)], own[len(chunks) :]
     buffers = [own[c * outer : (c + 1) * outer] for c in range(len(chunks))]
     for k in range(1, inner):
@@ -259,7 +269,7 @@
             tuple(made((count, share_y, lanes)) for _ in range(deep)),
             cost_y,
             scratch=(VMEM((2 * size_y, count * lanes), BF16),),
-        )(*[hold(parts[s]) for s in (0, *north_order)], *map(hold, table_y))
+        )(*[hold(parts[s]) for s in (0, *north_order)], hold(ready_y))
         sends_z = deep_sends(deep, c)
         steps_z = (0,) + tuple(s for s, _ in sends_z)
         gathered = [blocks[0]] + [lax.ppermute(blocks[s], "deep", pairs) for s, pairs in sends_z]

time: 45.4 us -> 45.4 us (level)
    unnamed x14 -> x10, local copies, waits for them, and re-layouts: 1.26 us -> 1.25 us
where the time goes in v3:
time: 45.4 us; the launch traced here: 45.2 us
  waiting for transfers between devices  23 us (51%)
  starting transfers between devices  14.5 us (32%)
  Pallas kernels  5.97 us (13%)
  local copies, waits for them, and re-layouts  1.39 us (3%)
    ppermute x6, waiting for transfers between devices, local(): lax.ppermute(blocks[s], 'deep', pairs)  13.5 us
    ppermute x6, waiting for transfers between devices, local(): parts[s] = lax.ppermute(parts[s], 'north', pairs)  8.46 us
    ppermute x6, starting transfers between devices, local(): lax.ppermute(blocks[s], 'deep', pairs)  7.41 us
    ppermute x6, starting transfers between devices, local(): parts[s] = lax.ppermute(parts[s], 'north', pairs)  7.11 us
    pallas_call x2, Pallas kernels, local(): call(functools.partial(z_kernel, fields, steps_z, deep, start), jax.Shape...  2.37 us
    pallas_call x1, Pallas kernels, local(): call(functools.partial(x_kernel, inner, outer, deep, spans), tuple(sends)...  1.8 us
    unnamed x10, local copies, waits for them, and re-layouts  1.25 us
    ppermute x1, waiting for transfers between devices, local(): taken = hold(lax.ppermute(field, 'north', pairs))  1.06 us
  transfers between devices with their start and end apart: 13, of which 6 were waited for; matrix products, arithmetic and copies ran while one was open for 1% of the time, Pallas kernels for 9%

profile of v3, /device:TPU:12, one launch (start us, length us, event | category | flops | bytes accessed | tf_op | source)
XLA Modules:
  0.0 45.2 jit_solution(7684187934220883881)
XLA Ops:
  0.0 0.0 collective-permute-start
  0.0 1.8 %shard_map.100 = (bf16[64,256]{1,0:T(8,128)(2,1)S(1)}, bf16[128,256]{1,0:T(8,128)(2,1)S(1)}, f32[96,128]{1,0:T(8,128)S(1)}, f32[96,128]{1,0:T(8,128)S(1)}, f32[9...) custom-call(f32[2,16,64,128]{3,2,1,0:T(8,128)} %bitcast.2, ...), custom_call_target="tpu_custom_call" | custom-call | flops 100663296 | bytes 2097152 | tf_op jit(solution)/shard_map/pallas_call | solution.py:238
  1.8 1.1 %collective-permute-done.refs_0_ = f32[2,16,64,128]{3,2,1,0:T(8,128)S(1)} collective-permute-done((f32[2,16,64,128]{3,2,1,0:T(8,128)}, f32[2,16,64,128]{3,2,1,0:T(8,128)S(1)}, u32[]{:S(2)}, u32[]{:S(2)}) %collective-permute-start) | collective-permute-done | bytes 1048608 | tf_op jit(solution)/shard_map/ppermute | solution.py:243
  2.9 0.5 %shard_map.104 = (f32[192,128]{1,0:T(8,128)S(1)}, f32[192,128]{1,0:T(8,128)S(1)}, f32[192,128]{1,0:T(8,128)S(1)}, f32[192,128]{1,0:T(8,128)S(1)}) custom-call(f32[2,16,64,128]{3,2,1,0:T(8,128)S(1)} %collective-permute-done.refs_0_, bf16[64,256]{1,0:T(8,128)(2,1)S(1)} %get-tuple-element.60.refs_1_, f32[96,128]{1,0:T(8,128)S(1)} %get-tuple-element.61.refs_2_, ...), custom_call_target="tpu_custom_call" | custom-call | flops 37748736 | bytes 2097152 | tf_op jit(solution)/shard_map/pallas_call | solution.py:246
  3.3 1.6 %collective-permute-start.7 = (f32[192,128]{1,0:T(8,128)S(1)}, f32[192,128]{1,0:T(8,128)S(1)}, u32[]{:S(2)}, u32[]{:S(2)}) collective-permute-start(f32[192,128]{1,0:T(8,128)S(1)} %get-tuple-element.66), channel_id=1, source_target_pairs={{0,8},{4,12},{8,0},{12,4},{16,24},{20,28},{24,16},{28,20},{1,9},{5... | collective-permute-start | bytes 294920 | tf_op jit(solution)/shard_map/ppermute | solution.py:265
  4.9 0.5 %shard_map.101 = (f32[160,128]{1,0:T(8,128)S(1)}, f32[160,128]{1,0:T(8,128)S(1)}, f32[160,128]{1,0:T(8,128)S(1)}, f32[160,128]{1,0:T(8,128)S(1)}) custom-call(f32[2,16,64,128]{3,2,1,0:T(8,128)S(1)} %collective-permute-done.refs_0_, bf16[128,256]{1,0:T(8,128)(2,1)S(1)} %get-tuple-element.43.refs_1_), custom_call_target="tpu_custom_call" | custom-call | flops 62914560 | bytes 2097152 | tf_op jit(solution)/shard_map/pallas_call | solution.py:246
  5.5 0.6 %collective-permute-start.1 = (f32[320,128]{1,0:T(8,128)S(1)}, f32[320,128]{1,0:T(8,128)S(1)}, u32[]{:S(2)}, u32[]{:S(2)}) collective-permute-start(f32[320,128]{1,0:T(8,128)S(1)} %get-tuple-element.49), channel_id=1, source_target_pairs={{0,8},{4,12},{8,0},{12,4},{16,24},{20,28},{24,16},{28,20},{1,9},{5... | collective-permute-start | bytes 491528 | tf_op jit(solution)/shard_map/ppermute | solution.py:265
  6.1 0.5 %collective-permute-start.2 = (f32[320,128]{1,0:T(8,128)S(1)}, f32[320,128]{1,0:T(8,128)S(1)}, u32[]{:S(2)}, u32[]{:S(2)}) collective-permute-start(f32[320,128]{1,0:T(8,128)S(1)} %get-tuple-element.50), channel_id=1, source_target_pairs={{0,16},{4,20},{8,24},{12,28},{16,0},{20,4},{24,8},{28,12},{1,17},{... | collective-permute-start | bytes 491528 | tf_op jit(solution)/shard_map/ppermute | solution.py:265
  6.6 2.4 %collective-permute-start.3 = (f32[320,128]{1,0:T(8,128)S(1)}, f32[320,128]{1,0:T(8,128)S(1)}, u32[]{:S(2)}, u32[]{:S(2)}) collective-permute-start(f32[320,128]{1,0:T(8,128)S(1)} %get-tuple-element.51), channel_id=1, source_target_pairs={{0,24},{4,28},{8,16},{12,20},{16,8},{20,12},{24,0},{28,4},{1,25},{... | collective-permute-start | bytes 491528 | tf_op jit(solution)/shard_map/ppermute | solution.py:265
  9.0 0.5 %collective-permute-start.8 = (f32[192,128]{1,0:T(8,128)S(1)}, f32[192,128]{1,0:T(8,128)S(1)}, u32[]{:S(2)}, u32[]{:S(2)}) collective-permute-start(f32[192,128]{1,0:T(8,128)S(1)} %get-tuple-element.67), channel_id=1, source_target_pairs={{0,16},{4,20},{8,24},{12,28},{16,0},{20,4},{24,8},{28,12},{1,17},{... | collective-permute-start | bytes 294920 | tf_op jit(solution)/shard_map/ppermute | solution.py:265
  9.5 0.0 collective-permute-done.7.refs_1_
  9.5 1.5 %collective-permute-start.9 = (f32[192,128]{1,0:T(8,128)S(1)}, f32[192,128]{1,0:T(8,128)S(1)}, u32[]{:S(2)}, u32[]{:S(2)}) collective-permute-start(f32[192,128]{1,0:T(8,128)S(1)} %get-tuple-element.68), channel_id=1, source_target_pairs={{0,24},{4,28},{8,16},{12,20},{16,8},{20,12},{24,0},{28,4},{1,25},{... | collective-permute-start | bytes 294920 | tf_op jit(solution)/shard_map/ppermute | solution.py:265
  11.0 8.4 %collective-permute-done.8.refs_2_ = f32[192,128]{1,0:T(8,128)S(1)} collective-permute-done((f32[192,128]{1,0:T(8,128)S(1)}, f32[192,128]{1,0:T(8,128)S(1)}, u32[]{:S(2)}, u32[]{:S(2)}) %collective-permute-start.8) | collective-permute-done | bytes 98336 | tf_op jit(solution)/shard_map/ppermute | solution.py:265
  19.5 0.0 collective-permute-done.9.refs_3_
  19.5 0.3 shard_map.105
  19.8 1.6 %collective-permute-start.10 = (f32[6,32,128]{2,1,0:T(8,128)S(1)}, f32[6,32,128]{2,1,0:T(8,128)S(1)}, u32[]{:S(2)}, u32[]{:S(2)}) collective-permute-start(f32[6,32,128]{2,1,0:T(8,128)S(1)} %get-tuple-element.70), channel_id=1, source_target_pairs={{0,3},{1,2},{2,1},{3,0},{4,7},{5,6},{6,5},{7,4},{8,11},{9,10},{10,... | collective-permute-start | bytes 294920 | tf_op jit(solution)/shard_map/ppermute | solution.py:275
  21.5 1.2 %collective-permute-start.11 = (f32[6,32,128]{2,1,0:T(8,128)S(1)}, f32[6,32,128]{2,1,0:T(8,128)S(1)}, u32[]{:S(2)}, u32[]{:S(2)}) collective-permute-start(f32[6,32,128]{2,1,0:T(8,128)S(1)} %get-tuple-element.71), channel_id=1, source_target_pairs={{0,2},{1,3},{2,0},{3,1},{4,6},{5,7},{6,4},{7,5},{8,10},{9,11},{10,... | collective-permute-start | bytes 294920 | tf_op jit(solution)/shard_map/ppermute | solution.py:275
  22.7 0.0 collective-permute-done.1.refs_1_
  22.7 1.2 %collective-permute-start.12 = (f32[6,32,128]{2,1,0:T(8,128)S(1)}, f32[6,32,128]{2,1,0:T(8,128)S(1)}, u32[]{:S(2)}, u32[]{:S(2)}) collective-permute-start(f32[6,32,128]{2,1,0:T(8,128)S(1)} %get-tuple-element.72), channel_id=1, source_target_pairs={{0,1},{1,0},{2,3},{3,2},{4,5},{5,4},{6,7},{7,6},{8,9},{9,8},{10,11... | collective-permute-start | bytes 294920 | tf_op jit(solution)/shard_map/ppermute | solution.py:275
  23.9 0.0 collective-permute-done.2.refs_2_
  23.9 0.0 collective-permute-done.3.refs_3_
  23.9 0.5 %shard_map.103 = (f32[10,32,128]{2,1,0:T(8,128)S(1)}, f32[10,32,128]{2,1,0:T(8,128)S(1)}, f32[10,32,128]{2,1,0:T(8,128)S(1)}, f32[10,32,128]{2,1,0:T(8,128)S(1)}) custom-call(f32[320,128]{1,0:T(8,128)S(1)} %get-tuple-element.48.refs_0_, f32[320,128]{1,0:T(8,128)S(1)} %collective-permute-done.1.refs_1_, f32[320,128]{1,0:T(8,128)S(1)} %collective-permute-done.2.refs_2_, ...), custom_call_target="tpu_custom_call" | custom-call | flops 125829120 | bytes 1310720 | tf_op jit(solution)/shard_map/pallas_call | solution.py:267
  24.4 3.0 %collective-permute-start.4 = (f32[10,32,128]{2,1,0:T(8,128)S(1)}, f32[10,32,128]{2,1,0:T(8,128)S(1)}, u32[]{:S(2)}, u32[]{:S(2)}) collective-permute-start(f32[10,32,128]{2,1,0:T(8,128)S(1)} %get-tuple-element.54), channel_id=1, source_target_pairs={{0,2},{1,3},{2,0},{3,1},{4,6},{5,7},{6,4},{7,5},{8,10},{9,11},{10,... | collective-permute-start | bytes 491528 | tf_op jit(solution)/shard_map/ppermute | solution.py:275
  27.4 0.0 collective-permute-start.5
  27.4 0.0 copy-start.3
  27.4 0.7 %copy-done.3 = f32[128]{0:T(128)S(1)} copy-done((f32[128]{0:T(128)S(1)}, f32[128]{0:T(128)}, u32[]{:S(2)}) %copy-start.3) | copy-done | bytes 536
  28.1 0.0 copy-start.4
  28.1 0.1 dynamic_slice.6
  28.1 0.6 %copy-done.4 = f32[128]{0:T(128)S(1)} copy-done((f32[128]{0:T(128)S(1)}, f32[128]{0:T(128)}, u32[]{:S(2)}) %copy-start.4) | copy-done | bytes 536
  28.7 0.1 dynamic_slice.7
  28.8 0.0 copy-start.2
  28.8 0.1 broadcast_add_fusion
  28.9 0.0 copy-start
  28.9 0.0 copy-start.1
  28.9 1.3 %collective-permute-done.10.refs_1_ = f32[6,32,128]{2,1,0:T(8,128)S(1)} collective-permute-done((f32[6,32,128]{2,1,0:T(8,128)S(1)}, f32[6,32,128]{2,1,0:T(8,128)S(1)}, u32[]{:S(2)}, u32[]{:S(2)}) %collective-permute-start.10) | collective-permute-done | bytes 98336 | tf_op jit(solution)/shard_map/ppermute | solution.py:275
  30.2 0.3 collective-permute-start.6
  30.5 0.0 copy-done.2
  30.5 0.2 add_divide_fusion.refs_6_
  30.7 6.9 %collective-permute-done.11.refs_2_ = f32[6,32,128]{2,1,0:T(8,128)S(1)} collective-permute-done((f32[6,32,128]{2,1,0:T(8,128)S(1)}, f32[6,32,128]{2,1,0:T(8,128)S(1)}, u32[]{:S(2)}, u32[]{:S(2)}) %collective-permute-start.11) | collective-permute-done | bytes 98336 | tf_op jit(solution)/shard_map/ppermute | solution.py:275
  37.5 0.0 collective-permute-done.12.refs_3_
  37.5 0.0 copy-done
  37.5 0.0 copy-done.1
  37.6 1.1 %shard_map.106.refs_7_ = f32[2,16,32,256]{3,2,1,0:T(8,128)} custom-call(f32[6,32,128]{2,1,0:T(8,128)S(1)} %get-tuple-element.69.refs_0_, f32[6,32,128]{2,1,0:T(8,128)S(1)} %collective-permute-done.10.refs_1_, f32[6,32,128]{2,1,0:T(8,128)S(1)} %collective-permute-done.11.refs_2_, f32[6,32,128]{2,1,0:T(8,128)S(1)} %collective-permute-done.12.refs_3_, ...), custom_call_target="tpu_custom_call" | custom-call | flops 150994944 | bytes 786432 | tf_op jit(solution)/shard_map/pallas_call | solution.py:291
  38.7 2.6 %collective-permute-done.4.refs_1_ = f32[10,32,128]{2,1,0:T(8,128)S(1)} collective-permute-done((f32[10,32,128]{2,1,0:T(8,128)S(1)}, f32[10,32,128]{2,1,0:T(8,128)S(1)}, u32[]{:S(2)}, u32[]{:S(2)}) %collective-permute-start.4) | collective-permute-done | bytes 163872 | tf_op jit(solution)/shard_map/ppermute | solution.py:275
  41.3 2.7 %collective-permute-done.5.refs_2_ = f32[10,32,128]{2,1,0:T(8,128)S(1)} collective-permute-done((f32[10,32,128]{2,1,0:T(8,128)S(1)}, f32[10,32,128]{2,1,0:T(8,128)S(1)}, u32[]{:S(2)}, u32[]{:S(2)}) %collective-permute-start.5) | collective-permute-done | bytes 163872 | tf_op jit(solution)/shard_map/ppermute | solution.py:275
  44.0 0.0 collective-permute-done.6.refs_3_
  44.0 1.2 %shard_map.107 = f32[2,16,32,256]{3,2,1,0:T(8,128)} custom-call(f32[10,32,128]{2,1,0:T(8,128)S(1)} %get-tuple-element.53.refs_0_, f32[10,32,128]{2,1,0:T(8,128)S(1)} %collective-permute-done.4.refs_1_, f32[10,32,128]{2,1,0:T(8,128)S(1)} %collective-permute-done.5.refs_2_, ...), custom_call_target="tpu_custom_call", output_to_operand_aliasing={{}: (7, {})} | custom-call | flops 251658240 | bytes 1310720 | tf_op jit(solution)/shard_map/pallas_call | solution.py:291
  (1 shorter events, 0.0 us)
Async XLA Ops:
  0.0 2.9 %collective-permute-start = (f32[2,16,64,128]{3,2,1,0:T(8,128)}, f32[2,16,64,128]{3,2,1,0:T(8,128)S(1)}, u32[]{:S(2)}, u32[]{:S(2)}) collective-permute-start(f32[2,16,64,128]{3,2,1,0:T(8,128)} %bitcast.1), channel_id=1, source_target_pairs={{0,4},{4,0},{8,12},{12,8},{16,20},{20,16},{24,28},{28,24},{1,5},{5... | collective-permute-start | bytes 3145736 | tf_op jit(solution)/shard_map/ppermute | solution.py:243
  3.3 6.2 %collective-permute-start.7 = (f32[192,128]{1,0:T(8,128)S(1)}, f32[192,128]{1,0:T(8,128)S(1)}, u32[]{:S(2)}, u32[]{:S(2)}) collective-permute-start(f32[192,128]{1,0:T(8,128)S(1)} %get-tuple-element.66), channel_id=1, source_target_pairs={{0,8},{4,12},{8,0},{12,4},{16,24},{20,28},{24,16},{28,20},{1,9},{5... | collective-permute-start | bytes 294920 | tf_op jit(solution)/shard_map/ppermute | solution.py:265
  5.5 17.2 %collective-permute-start.1 = (f32[320,128]{1,0:T(8,128)S(1)}, f32[320,128]{1,0:T(8,128)S(1)}, u32[]{:S(2)}, u32[]{:S(2)}) collective-permute-start(f32[320,128]{1,0:T(8,128)S(1)} %get-tuple-element.49), channel_id=1, source_target_pairs={{0,8},{4,12},{8,0},{12,4},{16,24},{20,28},{24,16},{28,20},{1,9},{5... | collective-permute-start | bytes 491528 | tf_op jit(solution)/shard_map/ppermute | solution.py:265
  6.1 17.9 %collective-permute-start.2 = (f32[320,128]{1,0:T(8,128)S(1)}, f32[320,128]{1,0:T(8,128)S(1)}, u32[]{:S(2)}, u32[]{:S(2)}) collective-permute-start(f32[320,128]{1,0:T(8,128)S(1)} %get-tuple-element.50), channel_id=1, source_target_pairs={{0,16},{4,20},{8,24},{12,28},{16,0},{20,4},{24,8},{28,12},{1,17},{... | collective-permute-start | bytes 491528 | tf_op jit(solution)/shard_map/ppermute | solution.py:265
  6.6 17.4 %collective-permute-start.3 = (f32[320,128]{1,0:T(8,128)S(1)}, f32[320,128]{1,0:T(8,128)S(1)}, u32[]{:S(2)}, u32[]{:S(2)}) collective-permute-start(f32[320,128]{1,0:T(8,128)S(1)} %get-tuple-element.51), channel_id=1, source_target_pairs={{0,24},{4,28},{8,16},{12,20},{16,8},{20,12},{24,0},{28,4},{1,25},{... | collective-permute-start | bytes 491528 | tf_op jit(solution)/shard_map/ppermute | solution.py:265
  9.0 10.5 %collective-permute-start.8 = (f32[192,128]{1,0:T(8,128)S(1)}, f32[192,128]{1,0:T(8,128)S(1)}, u32[]{:S(2)}, u32[]{:S(2)}) collective-permute-start(f32[192,128]{1,0:T(8,128)S(1)} %get-tuple-element.67), channel_id=1, source_target_pairs={{0,16},{4,20},{8,24},{12,28},{16,0},{20,4},{24,8},{28,12},{1,17},{... | collective-permute-start | bytes 294920 | tf_op jit(solution)/shard_map/ppermute | solution.py:265
  9.5 9.9 %collective-permute-start.9 = (f32[192,128]{1,0:T(8,128)S(1)}, f32[192,128]{1,0:T(8,128)S(1)}, u32[]{:S(2)}, u32[]{:S(2)}) collective-permute-start(f32[192,128]{1,0:T(8,128)S(1)} %get-tuple-element.68), channel_id=1, source_target_pairs={{0,24},{4,28},{8,16},{12,20},{16,8},{20,12},{24,0},{28,4},{1,25},{... | collective-permute-start | bytes 294920 | tf_op jit(solution)/shard_map/ppermute | solution.py:265
  19.8 10.3 %collective-permute-start.10 = (f32[6,32,128]{2,1,0:T(8,128)S(1)}, f32[6,32,128]{2,1,0:T(8,128)S(1)}, u32[]{:S(2)}, u32[]{:S(2)}) collective-permute-start(f32[6,32,128]{2,1,0:T(8,128)S(1)} %get-tuple-element.70), channel_id=1, source_target_pairs={{0,3},{1,2},{2,1},{3,0},{4,7},{5,6},{6,5},{7,4},{8,11},{9,10},{10,... | collective-permute-start | bytes 294920 | tf_op jit(solution)/shard_map/ppermute | solution.py:275
  21.5 16.1 %collective-permute-start.11 = (f32[6,32,128]{2,1,0:T(8,128)S(1)}, f32[6,32,128]{2,1,0:T(8,128)S(1)}, u32[]{:S(2)}, u32[]{:S(2)}) collective-permute-start(f32[6,32,128]{2,1,0:T(8,128)S(1)} %get-tuple-element.71), channel_id=1, source_target_pairs={{0,2},{1,3},{2,0},{3,1},{4,6},{5,7},{6,4},{7,5},{8,10},{9,11},{10,... | collective-permute-start | bytes 294920 | tf_op jit(solution)/shard_map/ppermute | solution.py:275
  22.7 14.9 %collective-permute-start.12 = (f32[6,32,128]{2,1,0:T(8,128)S(1)}, f32[6,32,128]{2,1,0:T(8,128)S(1)}, u32[]{:S(2)}, u32[]{:S(2)}) collective-permute-start(f32[6,32,128]{2,1,0:T(8,128)S(1)} %get-tuple-element.72), channel_id=1, source_target_pairs={{0,1},{1,0},{2,3},{3,2},{4,5},{5,4},{6,7},{7,6},{8,9},{9,8},{10,11... | collective-permute-start | bytes 294920 | tf_op jit(solution)/shard_map/ppermute | solution.py:275
  24.4 16.9 %collective-permute-start.4 = (f32[10,32,128]{2,1,0:T(8,128)S(1)}, f32[10,32,128]{2,1,0:T(8,128)S(1)}, u32[]{:S(2)}, u32[]{:S(2)}) collective-permute-start(f32[10,32,128]{2,1,0:T(8,128)S(1)} %get-tuple-element.54), channel_id=1, source_target_pairs={{0,2},{1,3},{2,0},{3,1},{4,6},{5,7},{6,4},{7,5},{8,10},{9,11},{10,... | collective-permute-start | bytes 491528 | tf_op jit(solution)/shard_map/ppermute | solution.py:275
  27.4 16.6 %collective-permute-start.5 = (f32[10,32,128]{2,1,0:T(8,128)S(1)}, f32[10,32,128]{2,1,0:T(8,128)S(1)}, u32[]{:S(2)}, u32[]{:S(2)}) collective-permute-start(f32[10,32,128]{2,1,0:T(8,128)S(1)} %get-tuple-element.55), channel_id=1, source_target_pairs={{0,3},{1,2},{2,1},{3,0},{4,7},{5,6},{6,5},{7,4},{8,11},{9,10},{10,... | collective-permute-start | bytes 491528 | tf_op jit(solution)/shard_map/ppermute | solution.py:275
  27.4 0.7 %copy-start.3 = (f32[128]{0:T(128)S(1)}, f32[128]{0:T(128)}, u32[]{:S(2)}) copy-start(f32[128]{0:T(128)} %param.11) | copy-start | bytes 1540
  28.1 0.7 %copy-start.4 = (f32[128]{0:T(128)S(1)}, f32[128]{0:T(128)}, u32[]{:S(2)}) copy-start(f32[128]{0:T(128)} %param.12) | copy-start | bytes 1540
  28.8 1.7 %copy-start.2 = (f32[256]{0:T(256)S(1)}, f32[256]{0:T(256)}, u32[]{:S(2)}) copy-start(f32[256]{0:T(256)} %param.13) | copy-start | bytes 3076
  28.9 8.7 %copy-start = (bf16[256,256]{1,0:T(8,128)(2,1)S(1)}, bf16[256,256]{1,0:T(8,128)(2,1)}, u32[]{:S(2)}) copy-start(bf16[256,256]{1,0:T(8,128)(2,1)} %constant.38.clone.refs_5_) | copy-start | bytes 393220
  28.9 8.7 %copy-start.1 = (bf16[256,256]{1,0:T(8,128)(2,1)S(1)}, bf16[256,256]{1,0:T(8,128)(2,1)}, u32[]{:S(2)}) copy-start(bf16[256,256]{1,0:T(8,128)(2,1)} %constant.37.clone.refs_4_) | copy-start | bytes 393220
  30.2 13.8 %collective-permute-start.6 = (f32[10,32,128]{2,1,0:T(8,128)S(1)}, f32[10,32,128]{2,1,0:T(8,128)S(1)}, u32[]{:S(2)}, u32[]{:S(2)}) collective-permute-start(f32[10,32,128]{2,1,0:T(8,128)S(1)} %get-tuple-element.56), channel_id=1, source_target_pairs={{0,1},{1,0},{2,3},{3,2},{4,5},{5,4},{6,7},{7,6},{8,9},{9,8},{10,11... | collective-permute-start | bytes 491528 | tf_op jit(solution)/shard_map/ppermute | solution.py:275
